TPU v7x, 32 devices: a whole 2x2x4 slice. The times are simulated.
32 devices in a mesh: seq: 2 (over core), chan: 4 (over y, x), batch: 4 (over z).
Axes of the slice: x: 2, y: 2, z: 4, core: 2. Of those that a mesh axis runs over, the one named last changes fastest.
Arguments:
- ssm_input: bfloat16 [8192, 4096], P(('batch', 'seq'), 'chan'), parts along dimension 0, may hold values from -6 to 6
- gate_z: bfloat16 [8192, 4096], P(('batch', 'seq'), 'chan'), parts along dimension 0, may hold values from -6 to 6
- proj_forward: bfloat16 [2, 8192, 128], P(None, ('batch', 'seq')), parts along dimension 1, may hold values from -2 to 2
- proj_backward: bfloat16 [2, 8192, 128], P(None, ('batch', 'seq')), parts along dimension 1, may hold values from -2 to 2
- step_raw: float32 [2, 64, 8192], P(None, 'chan', ('batch', 'seq')), parts along dimension 2, may hold values from -3 to 3
- head_params: float32 [2, 2, 64], P(None, None, 'chan'), may hold values from -4 to 1, as said below
- skip_gain: float32 [64], P('chan'), may hold values from 0.25 to 2
- norm_gain: float32 [4096], P('chan'), may hold values from 0.5 to 1.5
- out_weight: bfloat16 [4096, 2048], P(None, 'chan'), may hold values from -0.09375 to 0.09375
Outputs:
- mixed: bfloat16 [8192, 2048], P(('batch', 'seq'), 'chan'), parts along dimension 0
There are 4 independent parts, one for each index of `batch`. A program takes and returns all parts, laid end to end along the dimension named above; an argument that names none is the same for every part. Nothing has to cross between parts.
Inputs may be any that keep to these rules, and one draw needn't show every extreme that they name: `head_params`: index 0 of the second dimension holds positive decay rates, index 1 time-step biases.
All inputs are finite; a program needn't handle non-finite values.
Results may differ from a plain program's by a relative error of at most 0.0085.
Values may be sent and summed in bfloat16 or wider, within the bound.
A program may use at most 128 MiB of HBM per device.

v0:
```python
import functools

import jax
import jax.numpy as jnp
from jax import lax
from jax.experimental import pallas as pl
from jax.experimental.pallas import tpu as pltpu
from jax.sharding import PartitionSpec as P

Q = 128
LOG2E = 1.4426950408889634
F32, BF16 = jnp.float32, jnp.bfloat16


def nn(a, b):
    return lax.dot_general(a, b, (((1,), (0,)), ((), ())), preferred_element_type=F32)


def nt(a, b):
    return lax.dot_general(a, b, (((1,), (1,)), ((), ())), preferred_element_type=F32)


def tn(a, b):
    return lax.dot_general(a, b, (((0,), (0,)), ((), ())), preferred_element_type=F32)


def rates_of(raw, hp_ref, heads):
    v = raw + hp_ref[:, 1:2]
    dt = jnp.maximum(v, 0.0) + jnp.log1p(jnp.exp(-jnp.abs(v)))
    l2 = (-LOG2E) * hp_ref[:, 0:1] * dt
    r = lax.broadcasted_iota(jnp.int32, (Q, Q), 0)
    t = lax.broadcasted_iota(jnp.int32, (Q, Q), 1)
    up = (r <= t).astype(F32)
    down = (r >= t).astype(F32)
    cf = jnp.dot(l2, up, preferred_element_type=F32, precision=lax.Precision.HIGHEST)
    cb = jnp.dot(l2, down, preferred_element_type=F32, precision=lax.Precision.HIGHEST)
    forward = lax.broadcasted_iota(jnp.int32, l2.shape, 0) < heads
    cum = jnp.where(forward, cf, cb)
    total = jnp.sum(l2, axis=1, keepdims=True)
    return dt, cum, total, jnp.log2(dt) - cum


def columns_of(rows):
    used = sum(r.shape[0] for r in rows)
    if used < 128:
        rows = rows + [jnp.zeros((128 - used, Q), F32)]
    return jnp.concatenate(rows, axis=0).T


def halves(cols):
    hi = cols.astype(BF16)
    lo = (cols - hi.astype(F32)).astype(BF16)
    return jnp.concatenate([hi, lo], axis=1)


def fill_spread(spread_ref, groups, heads, width):
    for k, group in enumerate(groups):
        shape = spread_ref.shape[1:]
        j = lax.broadcasted_iota(jnp.int32, shape, 0) % 128
        head = lax.broadcasted_iota(jnp.int32, shape, 1) // width
        spread_ref[k] = jnp.where(j == group * heads + head, 1.0, 0.0).astype(BF16)


def states_kernel(
    heads, width, x_ref, bf_ref, bb_ref, raw_ref, hp_ref,
    entf_ref, entb_ref, dec_ref, end_ref, endb_ref, tot_ref, sf, sb, df, db, spread,
):
    blocks = x_ref.shape[0] // Q
    fill_spread(spread, (0, 1, 2, 3), heads, width)
    sf[...] = jnp.zeros_like(sf)
    sb[...] = jnp.zeros_like(sb)
    df[...] = jnp.ones_like(df)
    db[...] = jnp.ones_like(db)

    def step(i, _):
        k = blocks - 1 - i
        at_f = pl.multiple_of(i * Q, Q)
        at_b = pl.multiple_of(k * Q, Q)
        raw = jnp.concatenate(
            [raw_ref[:, pl.ds(at_f, Q)][:heads], raw_ref[:, pl.ds(at_b, Q)][heads:]], axis=0
        )
        dt, cum, total, rowt = rates_of(raw, hp_ref, heads)
        gain = jnp.broadcast_to(jnp.exp2(total), cum.shape)
        cols = halves(columns_of([jnp.exp2(total + rowt), gain]))
        for at, block, b_ref, ent, state, dec, place in (
            (at_f, i, bf_ref, entf_ref, sf, df, 0),
            (at_b, k, bb_ref, entb_ref, sb, db, 1),
        ):
            ent[block] = state[...].astype(BF16)
            dec_ref[block, pl.ds(8 * place, 8), :] = dec[...]
            weigh = nn(cols, spread[place])
            xw = (x_ref[pl.ds(at, Q), :].astype(F32) * weigh).astype(BF16)
            decay = nn(cols[:16], spread[2 + place])[:8]
            state[...] = state[...] * decay[:1] + tn(b_ref[pl.ds(at, Q), :], xw)
            dec[...] = dec[...] * decay
        return 0

    lax.fori_loop(0, blocks, step, 0)
    end_ref[...] = sf[...].astype(BF16)
    endb_ref[...] = sb[...].astype(BF16)
    tot_ref[pl.ds(0, 8), :] = df[...]
    tot_ref[pl.ds(8, 8), :] = db[...]


def outputs_kernel(
    heads, width, x_ref, z_ref, pf_ref, pb_ref, raw_ref, hp_ref, skip_ref, gain_ref,
    entf_ref, entb_ref, dec_ref, cf_ref, cb_ref, g_ref, sq_ref, spread, base,
):
    @pl.when(pl.program_id(0) == 0)
    def _():
        fill_spread(spread, (2, 3, 5), heads, width)

    dt, cum, total, rowt = rates_of(raw_ref[...], hp_ref, heads)
    cols = columns_of([cum, jnp.exp2(cum), dt])
    b_f, c_f, b_b, c_b = pf_ref[0], pf_ref[1], pb_ref[0], pb_ref[1]
    lane = lax.broadcasted_iota(jnp.int32, (Q, 128), 1)
    diag = jnp.sum(b_b.astype(F32) * c_b.astype(F32), axis=1, keepdims=True)
    here = (lane >= 5 * heads) & (lane < 6 * heads)
    wide = halves(jnp.where(here, cols * diag + skip_ref[...], cols))
    dec = dec_ref[0]
    ent_f = (entf_ref[0].astype(F32) + dec[0:1] * cf_ref[...].astype(F32)).astype(BF16)
    ent_b = (entb_ref[0].astype(F32) + dec[8:9] * cb_ref[...].astype(F32)).astype(BF16)
    base[...] = nn(wide, spread[0]) * nn(c_f, ent_f)
    base[...] += nn(wide, spread[1]) * nn(c_b, ent_b)
    base[...] += nn(wide, spread[2]) * x_ref[...].astype(F32)

    t = lax.broadcasted_iota(jnp.int32, (Q, Q), 0)
    s = lax.broadcasted_iota(jnp.int32, (Q, Q), 1)
    lower = s <= t
    scores = jnp.where(lower, nt(c_f, b_f), nt(c_b, b_b))
    per = 128 // width
    squares = jnp.zeros((Q, 128), F32)
    for group in range(heads // per):
        lanes = slice(group * 128, (group + 1) * 128)
        x = x_ref[:, lanes]
        weights, values = [], []
        for k in range(per):
            h = group * per + k
            gap_f = cols[:, h : h + 1] + rowt[h : h + 1, :]
            gap_b = cols[:, heads + h : heads + h + 1] + rowt[heads + h : heads + h + 1, :]
            weights.append((scores * jnp.exp2(jnp.where(lower, gap_f, gap_b))).astype(BF16))
            own = (lane >= k * width) & (lane < (k + 1) * width)
            values.append(jnp.where(own, x, jnp.zeros_like(x)))
        intra = nn(jnp.concatenate(weights, axis=1), jnp.concatenate(values, axis=0))
        z = z_ref[:, lanes].astype(F32)
        gated = (base[:, lanes] + intra) * (z / (1.0 + jnp.exp(-z)))
        squares += gated * gated
        g_ref[:, lanes] = (gated * gain_ref[:, lanes]).astype(BF16)
    sums = jnp.sum(squares.T, axis=0, keepdims=True)
    sq_ref[...] = jnp.broadcast_to(sums, sq_ref.shape)


def body(
    ssm_input, gate_z, proj_forward, proj_backward, step_raw, head_params,
    skip_gain, norm_gain, out_weight,
):
    frames, inner = ssm_input.shape
    heads = step_raw.shape[1]
    width = inner // heads
    state = proj_forward.shape[2]
    blocks = frames // Q
    features = out_weight.shape[1]
    n_chan, n_seq = lax.axis_size("chan"), lax.axis_size("seq")
    chan, seq = lax.axis_index("chan"), lax.axis_index("seq")
    all_channels = inner * n_chan

    paired = n_chan & (n_chan - 1) == 0

    def partner(i, k):
        return i ^ k if paired else (i + k) % n_chan

    def source(i, k):
        return i ^ k if paired else (i + n_chan - k) % n_chan

    share = inner // n_seq
    pieces = {}
    for k in range(1, n_chan):
        start = partner(chan, k) * inner + seq * share
        part = lax.dynamic_slice(out_weight, (start, 0), (share, features))
        pieces[k] = lax.ppermute(part, "chan", [(i, partner(i, k)) for i in range(n_chan)])
    weights = {0: lax.dynamic_slice(out_weight, (chan * inner, 0), (inner, features))}
    for k in range(1, n_chan):
        whole = jnp.zeros((inner, features), out_weight.dtype)
        whole = lax.dynamic_update_slice(whole, pieces[k], (seq * share, 0))
        for j in range(1, n_seq):
            got = lax.ppermute(pieces[k], "seq", [(i, (i + j) % n_seq) for i in range(n_seq)])
            whole = lax.dynamic_update_slice(whole, got, (((seq + n_seq - j) % n_seq) * share, 0))
        weights[k] = whole

    raw = step_raw.reshape(2 * heads, frames)
    params = jnp.stack([head_params[:, 0].reshape(-1), head_params[:, 1].reshape(-1)], axis=1)
    skip_row = jnp.zeros((1, 128), F32)
    skip_row = lax.dynamic_update_slice(skip_row, skip_gain[None], (0, 5 * heads))
    gain_row = norm_gain[None]

    ent_f, ent_b, dec, end_f, end_b, tot = pl.pallas_call(
        functools.partial(states_kernel, heads, width),
        out_shape=(
            jax.ShapeDtypeStruct((blocks, state, inner), BF16),
            jax.ShapeDtypeStruct((blocks, state, inner), BF16),
            jax.ShapeDtypeStruct((blocks, 16, inner), F32),
            jax.ShapeDtypeStruct((state, inner), BF16),
            jax.ShapeDtypeStruct((state, inner), BF16),
            jax.ShapeDtypeStruct((16, inner), F32),
        ),
        scratch_shapes=[
            pltpu.VMEM((state, inner), F32),
            pltpu.VMEM((state, inner), F32),
            pltpu.VMEM((8, inner), F32),
            pltpu.VMEM((8, inner), F32),
            pltpu.VMEM((4, 256, inner), BF16),
        ],
        compiler_params=pltpu.CompilerParams(vmem_limit_bytes=40 * 2**20),
        cost_estimate=pl.CostEstimate(
            flops=4 * 10**9, bytes_accessed=8 * 2**20, transcendentals=0
        ),
        name="scan_states",
    )(ssm_input, proj_forward[0], proj_backward[0], raw, params)

    def carried(end, decay, step):
        pairs = [(i, i + step) for i in range(n_seq) if 0 <= i + step < n_seq]
        out = lax.ppermute(end, "seq", pairs)
        for _ in range(n_seq - 2):
            new = (end.astype(F32) + decay * out.astype(F32)).astype(BF16)
            out = lax.ppermute(new, "seq", pairs)
        return out

    carry_f = carried(end_f, tot[0:1], 1)
    carry_b = carried(end_b, tot[8:9], -1)

    chunks = 2 if blocks % 2 == 0 else 1
    count = blocks // chunks
    received = []
    for chunk in range(chunks):
        at = chunk * count
        rows = lambda i, at=at: (i + at, 0)
        rows3 = lambda i, at=at: (0, i + at, 0)
        block3 = lambda i, at=at: (i + at, 0, 0)
        same = lambda i: (0, 0)
        gated, sums = pl.pallas_call(
            functools.partial(outputs_kernel, heads, width),
            grid=(count,),
            in_specs=[
                pl.BlockSpec((Q, inner), rows),
                pl.BlockSpec((Q, inner), rows),
                pl.BlockSpec((2, Q, state), rows3),
                pl.BlockSpec((2, Q, state), rows3),
                pl.BlockSpec((2 * heads, Q), lambda i, at=at: (0, i + at)),
                pl.BlockSpec((2 * heads, 2), same),
                pl.BlockSpec((1, 128), same),
                pl.BlockSpec((1, inner), same),
                pl.BlockSpec((1, state, inner), block3),
                pl.BlockSpec((1, state, inner), block3),
                pl.BlockSpec((1, 16, inner), block3),
                pl.BlockSpec((state, inner), same),
                pl.BlockSpec((state, inner), same),
            ],
            out_specs=(
                pl.BlockSpec((Q, inner), lambda i: (i, 0)),
                pl.BlockSpec((8, Q), lambda i: (0, i)),
            ),
            out_shape=(
                jax.ShapeDtypeStruct((count * Q, inner), BF16),
                jax.ShapeDtypeStruct((8, count * Q), F32),
            ),
            scratch_shapes=[pltpu.VMEM((3, 256, inner), BF16), pltpu.VMEM((Q, inner), F32)],
            compiler_params=pltpu.CompilerParams(
                vmem_limit_bytes=40 * 2**20, dimension_semantics=("arbitrary",)
            ),
            cost_estimate=pl.CostEstimate(
                flops=4 * 10**9, bytes_accessed=8 * 2**20, transcendentals=0
            ),
            name="scan_outputs",
        )(
            ssm_input, gate_z, proj_forward, proj_backward, raw, params, skip_row, gain_row,
            ent_f, ent_b, dec, carry_f, carry_b,
        )
        sums = sums[0:1]
        squares = sums
        got = []
        for k in range(1, n_chan):
            perm = [(i, partner(i, k)) for i in range(n_chan)]
            kin = k if paired else n_chan - k
            part = jnp.dot(gated, weights[kin], preferred_element_type=F32).astype(BF16)
            got.append(lax.ppermute(part, "chan", perm))
            squares = squares + lax.ppermute(sums, "chan", perm)
        own = jnp.dot(gated, weights[0], preferred_element_type=F32)
        for part in got:
            own = own + part.astype(F32)
        scale = lax.rsqrt(squares[0] / all_channels + 1.0)
        received.append((own * scale[:, None]).astype(BF16))
    return jnp.concatenate(received, axis=0)


def solution(mesh):
    in_specs = (
        P(("batch", "seq"), "chan"),
        P(("batch", "seq"), "chan"),
        P(None, ("batch", "seq"), None),
        P(None, ("batch", "seq"), None),
        P(None, "chan", ("batch", "seq")),
        P(None, None, "chan"),
        P("chan"),
        P("chan"),
        P(None, "chan"),
    )
    out_specs = P(("batch", "seq"), "chan")
    return jax.shard_map(body, mesh=mesh, in_specs=in_specs, out_specs=out_specs, check_vma=False)
```

profile of v0, /device:TPU:0, one launch (start us, length us, event | category | flops | bytes accessed | tf_op | source)
XLA Modules:
  0.0 124.4 jit_solution(2687829437597288414)
XLA Ops:
  1.0 1.1 slice_bitcast_fusion
  2.1 1.6 %copy-done.2 = bf16[1024,1024]{1,0:T(8,128)(2,1)S(1)} copy-done((bf16[1024,1024]{1,0:T(8,128)(2,1)S(1)}, bf16[1024,1024]{1,0:T(8,128)(2,1)}, u32[]{:S(2)}) %copy-start.2) | copy-done | bytes 2097176
  4.6 9.1 %scan_states.1 = (bf16[8,128,1024]{2,1,0:T(8,128)(2,1)S(1)}, bf16[8,128,1024]{2,1,0:T(8,128)(2,1)S(1)}, f32[8,16,1024]{2,1,0:T(8,128)S(1)}, bf16[128,1024]{1,0:T...) custom-call(bf16[1024,1024]{1,0:T(8,128)(2,1)S(1)} %copy-done.2, ...), custom_call_target="tpu_custom_call" | custom-call | flops 4000000000 | bytes 8388608 | tf_op jit(solution)/shard_map/scan_states/pallas_call | solution.py:196
  13.7 1.4 %copy-done.12 = bf16[8,128,1024]{2,1,0:T(8,128)(2,1)} copy-done((bf16[8,128,1024]{2,1,0:T(8,128)(2,1)}, bf16[8,128,1024]{2,1,0:T(8,128)(2,1)S(1)}, u32[]{:S(2)}) %copy-start.12) | copy-done | bytes 2097176
  15.1 1.3 %copy-done.15 = bf16[8,128,1024]{2,1,0:T(8,128)(2,1)} copy-done((bf16[8,128,1024]{2,1,0:T(8,128)(2,1)}, bf16[8,128,1024]{2,1,0:T(8,128)(2,1)S(1)}, u32[]{:S(2)}) %copy-start.15) | copy-done | bytes 2097176
  17.2 2.7 %collective-permute-start = (bf16[128,1024]{1,0:T(8,128)(2,1)}, bf16[128,1024]{1,0:T(8,128)(2,1)S(1)}, u32[]{:S(2)}, u32[]{:S(2)}) collective-permute-start(bf16[128,1024]{1,0:T(8,128)(2,1)} %get-tuple-element.17), channel_id=1, source_target_pairs={{0,16},{1,17},{2,18},{3,19},{4,20},{5,21},{6,22},{7,23},{8,24},{9,... | collective-permute-start | bytes 786440 | tf_op jit(solution)/shard_map/ppermute | solution.py:222
  19.9 1.3 %collective-permute-start.1 = (bf16[128,1024]{1,0:T(8,128)(2,1)}, bf16[128,1024]{1,0:T(8,128)(2,1)}, u32[]{:S(2)}, u32[]{:S(2)}) collective-permute-start(bf16[128,1024]{1,0:T(8,128)(2,1)} %get-tuple-element.18), channel_id=1, source_target_pairs={{16,0},{17,1},{18,2},{19,3},{20,4},{21,5},{22,6},{23,7},{24,8},{25... | collective-permute-start | bytes 786440 | tf_op jit(solution)/shard_map/ppermute | solution.py:222
  21.2 2.6 %constant_dynamic-slice_fusion.2 = (bf16[512,512]{1,0:T(8,128)(2,1)}, bf16[512,512]{1,0:T(8,128)(2,1)}, bf16[512,512]{1,0:T(8,128)(2,1)}) fusion(bf16[4096,512]{1,0:T(8,128)(2,1)} %param.17, s32[]{:T(128)S(6)} %select_n.34, s32[]{:T(128)S(6)} %select_n.39, s32[]{:T(128)S(6)} %select_n.38), kind=kLoop, calls=%fused_computation.30 | loop fusion | bytes 3145740 | tf_op jit(solution)/shard_map/dynamic_slice | solution.py:179
  23.8 3.3 %collective-permute-start.8 = (bf16[512,512]{1,0:T(8,128)(2,1)}, bf16[512,512]{1,0:T(8,128)(2,1)}, u32[]{:S(2)}, u32[]{:S(2)}) collective-permute-start(bf16[512,512]{1,0:T(8,128)(2,1)} %get-tuple-element.26), channel_id=1, source_target_pairs={{0,12},{4,8},{8,4},{12,0},{1,13},{5,9},{9,5},{13,1},{2,14},{6,10},... | collective-permute-start | bytes 1572872 | tf_op jit(solution)/shard_map/ppermute | solution.py:180
  27.2 1.6 %copy-done.4 = bf16[1024,1024]{1,0:T(8,128)(2,1)S(1)} copy-done((bf16[1024,1024]{1,0:T(8,128)(2,1)S(1)}, bf16[1024,1024]{1,0:T(8,128)(2,1)}, u32[]{:S(2)}) %copy-start.4) | copy-done | bytes 2097176
  29.7 1.6 %copy-done.13 = bf16[8,128,1024]{2,1,0:T(8,128)(2,1)S(1)} copy-done((bf16[8,128,1024]{2,1,0:T(8,128)(2,1)S(1)}, bf16[8,128,1024]{2,1,0:T(8,128)(2,1)}, u32[]{:S(2)}) %copy-start.13) | copy-done | bytes 2097176
  31.3 1.6 %copy-done.16 = bf16[8,128,1024]{2,1,0:T(8,128)(2,1)S(1)} copy-done((bf16[8,128,1024]{2,1,0:T(8,128)(2,1)S(1)}, bf16[8,128,1024]{2,1,0:T(8,128)(2,1)}, u32[]{:S(2)}) %copy-start.16) | copy-done | bytes 2097176
  33.9 7.7 %scan_outputs.2 = (bf16[512,1024]{1,0:T(8,128)(2,1)S(1)}, f32[8,512]{1,0:T(8,128)S(1)}) custom-call(bf16[1024,1024]{1,0:T(8,128)(2,1)S(1)} %copy-done.3, bf16[1024,1024]{1,0:T(8,128)(2,1)S(1)} %copy-done.4, bf16[2,1024,128]{2,1,0:T(8,128)(2,1)S(1)} %copy-done, bf16[2,1024,128]{2,1,0:T(8,128)(2,1)S(1)} %copy-done.1, f32[32,1024]{1,0:T(8,128)S(1)} %bitcast.24, ...), custom_call_target="tpu_custom_call" | custom-call | flops 4000000000 | bytes 8388608 | tf_op jit(solution)/shard_map/scan_outputs/pallas_call | solution.py:240
  43.1 2.0 %collective-permute-start.5 = (bf16[512,512]{1,0:T(8,128)(2,1)}, bf16[512,512]{1,0:T(8,128)(2,1)}, u32[]{:S(2)}, u32[]{:S(2)}) collective-permute-start(bf16[512,512]{1,0:T(8,128)(2,1)} %get-tuple-element.27), channel_id=1, source_target_pairs={{0,8},{4,12},{8,0},{12,4},{1,9},{5,13},{9,1},{13,5},{2,10},{6,14},... | collective-permute-start | bytes 1572872 | tf_op jit(solution)/shard_map/ppermute | solution.py:180
  45.1 1.4 %collective-permute-start.13 = (f32[1,512]{1,0:T(1,128)S(1)}, f32[1,512]{1,0:T(1,128)S(1)}, u32[]{:S(2)}, u32[]{:S(2)}) collective-permute-start(f32[1,512]{1,0:T(1,128)S(1)} %slice.22), channel_id=1, source_target_pairs={{0,12},{4,8},{8,4},{12,0},{1,13},{5,9},{9,5},{13,1},{2,14},{6,10},... | collective-permute-start | bytes 6152 | tf_op jit(solution)/shard_map/ppermute | solution.py:286
  46.7 1.6 %copy-done.5 = bf16[1024,1024]{1,0:T(8,128)(2,1)S(1)} copy-done((bf16[1024,1024]{1,0:T(8,128)(2,1)S(1)}, bf16[1024,1024]{1,0:T(8,128)(2,1)}, u32[]{:S(2)}) %copy-start.5) | copy-done | bytes 2097176
  49.2 1.6 %copy-done.14 = bf16[8,128,1024]{2,1,0:T(8,128)(2,1)S(1)} copy-done((bf16[8,128,1024]{2,1,0:T(8,128)(2,1)S(1)}, bf16[8,128,1024]{2,1,0:T(8,128)(2,1)}, u32[]{:S(2)}) %copy-start.14) | copy-done | bytes 2097176
  50.8 1.6 %copy-done.17 = bf16[8,128,1024]{2,1,0:T(8,128)(2,1)S(1)} copy-done((bf16[8,128,1024]{2,1,0:T(8,128)(2,1)S(1)}, bf16[8,128,1024]{2,1,0:T(8,128)(2,1)}, u32[]{:S(2)}) %copy-start.17) | copy-done | bytes 2097176
  52.4 1.0 copy-done.20
  53.4 7.6 %scan_outputs.3 = (bf16[512,1024]{1,0:T(8,128)(2,1)S(1)}, f32[8,512]{1,0:T(8,128)S(1)}) custom-call(bf16[1024,1024]{1,0:T(8,128)(2,1)S(1)} %copy-done.3, bf16[1024,1024]{1,0:T(8,128)(2,1)S(1)} %copy-done.5, bf16[2,1024,128]{2,1,0:T(8,128)(2,1)S(1)} %copy-done, bf16[2,1024,128]{2,1,0:T(8,128)(2,1)S(1)} %copy-done.1, f32[32,1024]{1,0:T(8,128)S(1)} %bitcast.25, ...), custom_call_target="tpu_custom_call" | custom-call | flops 4000000000 | bytes 8388608 | tf_op jit(solution)/shard_map/scan_outputs/pallas_call | solution.py:240
  61.1 2.0 %collective-permute-start.18 = (f32[1,512]{1,0:T(1,128)S(1)}, f32[1,512]{1,0:T(1,128)S(1)}, u32[]{:S(2)}, u32[]{:S(2)}) collective-permute-start(f32[1,512]{1,0:T(1,128)S(1)} %slice.23), channel_id=1, source_target_pairs={{0,8},{4,12},{8,0},{12,4},{1,9},{5,13},{9,1},{13,5},{2,10},{6,14},... | collective-permute-start | bytes 6152 | tf_op jit(solution)/shard_map/ppermute | solution.py:286
  63.1 1.4 %collective-permute-start.19 = (f32[1,512]{1,0:T(1,128)S(1)}, f32[1,512]{1,0:T(1,128)S(1)}, u32[]{:S(2)}, u32[]{:S(2)}) collective-permute-start(f32[1,512]{1,0:T(1,128)S(1)} %slice.23), channel_id=1, source_target_pairs={{0,12},{4,8},{8,4},{12,0},{1,13},{5,9},{9,5},{13,1},{2,14},{6,10},... | collective-permute-start | bytes 6152 | tf_op jit(solution)/shard_map/ppermute | solution.py:286
  65.3 1.1 constant_dynamic-update-slice_fusion.5
  66.5 1.1 constant_dynamic-update-slice_fusion.1
  67.6 1.1 constant_dynamic-update-slice_fusion.3
  72.4 1.9 %collective-permute-start.7 = (bf16[512,512]{1,0:T(8,128)(2,1)S(1)}, bf16[512,512]{1,0:T(8,128)(2,1)S(1)}, u32[]{:S(2)}, u32[]{:S(2)}) collective-permute-start(bf16[512,512]{1,0:T(8,128)(2,1)S(1)} %convolution_convert_fusion.4), channel_id=1, source_target_pairs={{0,8},{4,12},{8,0},{12,4},{1,9},{5,13},{9,1},{13,5},{2,10},{6,14},... | collective-permute-start | bytes 1572872 | tf_op jit(solution)/shard_map/ppermute | solution.py:285
  74.3 1.4 %collective-permute-start.10 = (bf16[512,512]{1,0:T(8,128)(2,1)S(1)}, bf16[512,512]{1,0:T(8,128)(2,1)S(1)}, u32[]{:S(2)}, u32[]{:S(2)}) collective-permute-start(bf16[512,512]{1,0:T(8,128)(2,1)S(1)} %convolution_convert_fusion.3), channel_id=1, source_target_pairs={{0,12},{4,8},{8,4},{12,0},{1,13},{5,9},{9,5},{13,1},{2,14},{6,10},... | collective-permute-start | bytes 1572872 | tf_op jit(solution)/shard_map/ppermute | solution.py:285
  77.4 2.0 %collective-permute-start.14 = (bf16[512,512]{1,0:T(8,128)(2,1)S(1)}, bf16[512,512]{1,0:T(8,128)(2,1)S(1)}, u32[]{:S(2)}, u32[]{:S(2)}) collective-permute-start(bf16[512,512]{1,0:T(8,128)(2,1)S(1)} %convolution_convert_fusion.2), channel_id=1, source_target_pairs={{0,4},{4,0},{8,12},{12,8},{1,5},{5,1},{9,13},{13,9},{2,6},{6,2},{1... | collective-permute-start | bytes 1572872 | tf_op jit(solution)/shard_map/ppermute | solution.py:285
  79.4 19.0 %collective-permute-done.17 = f32[1,512]{1,0:T(1,128)S(1)} collective-permute-done((f32[1,512]{1,0:T(1,128)S(1)}, f32[1,512]{1,0:T(1,128)S(1)}, u32[]{:S(2)}, u32[]{:S(2)}) %collective-permute-start.17) | collective-permute-done | bytes 2080 | tf_op jit(solution)/shard_map/ppermute | solution.py:286
  98.4 1.5 %collective-permute-start.15 = (bf16[512,512]{1,0:T(8,128)(2,1)S(1)}, bf16[512,512]{1,0:T(8,128)(2,1)S(1)}, u32[]{:S(2)}, u32[]{:S(2)}) collective-permute-start(bf16[512,512]{1,0:T(8,128)(2,1)S(1)} %convolution_convert_fusion.1), channel_id=1, source_target_pairs={{0,8},{4,12},{8,0},{12,4},{1,9},{5,13},{9,1},{13,5},{2,10},{6,14},... | collective-permute-start | bytes 1572872 | tf_op jit(solution)/shard_map/ppermute | solution.py:285
  100.9 8.7 %collective-permute-done.14 = bf16[512,512]{1,0:T(8,128)(2,1)S(1)} collective-permute-done((bf16[512,512]{1,0:T(8,128)(2,1)S(1)}, bf16[512,512]{1,0:T(8,128)(2,1)S(1)}, u32[]{:S(2)}, u32[]{:S(2)}) %collective-permute-start.14) | collective-permute-done | bytes 524320 | tf_op jit(solution)/shard_map/ppermute | solution.py:285
  109.7 12.9 %collective-permute-done.15 = bf16[512,512]{1,0:T(8,128)(2,1)S(1)} collective-permute-done((bf16[512,512]{1,0:T(8,128)(2,1)S(1)}, bf16[512,512]{1,0:T(8,128)(2,1)S(1)}, u32[]{:S(2)}, u32[]{:S(2)}) %collective-permute-start.15) | collective-permute-done | bytes 524320 | tf_op jit(solution)/shard_map/ppermute | solution.py:285
  (87 shorter events, 16.4 us)
Async XLA Ops:
  2.1 1.6 %copy-start.2 = (bf16[1024,1024]{1,0:T(8,128)(2,1)S(1)}, bf16[1024,1024]{1,0:T(8,128)(2,1)}, u32[]{:S(2)}) copy-start(bf16[1024,1024]{1,0:T(8,128)(2,1)} %x_ref.5) | copy-start | bytes 6291460
  17.2 9.9 %copy-start.22 = (f32[16]{0:T(128)S(1)}, f32[16]{0:T(128)}, u32[]{:S(2)}) copy-start(f32[16]{0:T(128)} %param.15) | copy-start | bytes 196
  17.2 10.0 %copy-start = (bf16[2,1024,128]{2,1,0:T(8,128)(2,1)S(1)}, bf16[2,1024,128]{2,1,0:T(8,128)(2,1)}, u32[]{:S(2)}) copy-start(bf16[2,1024,128]{2,1,0:T(8,128)(2,1)} %pf_ref.3) | copy-start | bytes 1572868
  17.2 10.0 %copy-start.1 = (bf16[2,1024,128]{2,1,0:T(8,128)(2,1)S(1)}, bf16[2,1024,128]{2,1,0:T(8,128)(2,1)}, u32[]{:S(2)}) copy-start(bf16[2,1024,128]{2,1,0:T(8,128)(2,1)} %pb_ref.3) | copy-start | bytes 1572868
  17.2 10.0 %copy-start.3 = (bf16[1024,1024]{1,0:T(8,128)(2,1)S(1)}, bf16[1024,1024]{1,0:T(8,128)(2,1)}, u32[]{:S(2)}) copy-start(bf16[1024,1024]{1,0:T(8,128)(2,1)} %x_ref.5) | copy-start | bytes 6291460
  17.2 10.0 %copy-start.9 = (f32[1024]{0:T(1024)S(1)}, f32[1024]{0:T(1024)}, u32[]{:S(2)}) copy-start(f32[1024]{0:T(1024)} %param.16) | copy-start | bytes 12292
  17.2 10.0 %collective-permute-start = (bf16[128,1024]{1,0:T(8,128)(2,1)}, bf16[128,1024]{1,0:T(8,128)(2,1)S(1)}, u32[]{:S(2)}, u32[]{:S(2)}) collective-permute-start(bf16[128,1024]{1,0:T(8,128)(2,1)} %get-tuple-element.17), channel_id=1, source_target_pairs={{0,16},{1,17},{2,18},{3,19},{4,20},{5,21},{6,22},{7,23},{8,24},{9,... | collective-permute-start | bytes 786440 | tf_op jit(solution)/shard_map/ppermute | solution.py:222
  19.9 7.3 %collective-permute-start.1 = (bf16[128,1024]{1,0:T(8,128)(2,1)}, bf16[128,1024]{1,0:T(8,128)(2,1)}, u32[]{:S(2)}, u32[]{:S(2)}) collective-permute-start(bf16[128,1024]{1,0:T(8,128)(2,1)} %get-tuple-element.18), channel_id=1, source_target_pairs={{16,0},{17,1},{18,2},{19,3},{20,4},{21,5},{22,6},{23,7},{24,8},{25... | collective-permute-start | bytes 786440 | tf_op jit(solution)/shard_map/ppermute | solution.py:222
  23.8 40.7 %collective-permute-start.8 = (bf16[512,512]{1,0:T(8,128)(2,1)}, bf16[512,512]{1,0:T(8,128)(2,1)}, u32[]{:S(2)}, u32[]{:S(2)}) collective-permute-start(bf16[512,512]{1,0:T(8,128)(2,1)} %get-tuple-element.26), channel_id=1, source_target_pairs={{0,12},{4,8},{8,4},{12,0},{1,13},{5,9},{9,5},{13,1},{2,14},{6,10},... | collective-permute-start | bytes 1572872 | tf_op jit(solution)/shard_map/ppermute | solution.py:180
  27.2 1.6 %copy-start.4 = (bf16[1024,1024]{1,0:T(8,128)(2,1)S(1)}, bf16[1024,1024]{1,0:T(8,128)(2,1)}, u32[]{:S(2)}) copy-start(bf16[1024,1024]{1,0:T(8,128)(2,1)} %z_ref.3) | copy-start | bytes 6291460
  29.7 1.6 %copy-start.13 = (bf16[8,128,1024]{2,1,0:T(8,128)(2,1)S(1)}, bf16[8,128,1024]{2,1,0:T(8,128)(2,1)}, u32[]{:S(2)}) copy-start(bf16[8,128,1024]{2,1,0:T(8,128)(2,1)} %copy-done.12) | copy-start | bytes 6291460
  42.6 4.0 %collective-permute-start.12 = (f32[1,512]{1,0:T(1,128)S(1)}, f32[1,512]{1,0:T(1,128)S(1)}, u32[]{:S(2)}, u32[]{:S(2)}) collective-permute-start(f32[1,512]{1,0:T(1,128)S(1)} %slice.22), channel_id=1, source_target_pairs={{0,8},{4,12},{8,0},{12,4},{1,9},{5,13},{9,1},{13,5},{2,10},{6,14},... | collective-permute-start | bytes 6152 | tf_op jit(solution)/shard_map/ppermute | solution.py:286
  43.1 21.5 %collective-permute-start.2 = (bf16[512,512]{1,0:T(8,128)(2,1)}, bf16[512,512]{1,0:T(8,128)(2,1)}, u32[]{:S(2)}, u32[]{:S(2)}) collective-permute-start(bf16[512,512]{1,0:T(8,128)(2,1)} %get-tuple-element.25), channel_id=1, source_target_pairs={{0,4},{4,0},{8,12},{12,8},{1,5},{5,1},{9,13},{13,9},{2,6},{6,2},{1... | collective-permute-start | bytes 1572872 | tf_op jit(solution)/shard_map/ppermute | solution.py:180
  43.1 22.0 %collective-permute-start.5 = (bf16[512,512]{1,0:T(8,128)(2,1)}, bf16[512,512]{1,0:T(8,128)(2,1)}, u32[]{:S(2)}, u32[]{:S(2)}) collective-permute-start(bf16[512,512]{1,0:T(8,128)(2,1)} %get-tuple-element.27), channel_id=1, source_target_pairs={{0,8},{4,12},{8,0},{12,4},{1,9},{5,13},{9,1},{13,5},{2,10},{6,14},... | collective-permute-start | bytes 1572872 | tf_op jit(solution)/shard_map/ppermute | solution.py:180
  45.1 16.0 %collective-permute-start.13 = (f32[1,512]{1,0:T(1,128)S(1)}, f32[1,512]{1,0:T(1,128)S(1)}, u32[]{:S(2)}, u32[]{:S(2)}) collective-permute-start(f32[1,512]{1,0:T(1,128)S(1)} %slice.22), channel_id=1, source_target_pairs={{0,12},{4,8},{8,4},{12,0},{1,13},{5,9},{9,5},{13,1},{2,14},{6,10},... | collective-permute-start | bytes 6152 | tf_op jit(solution)/shard_map/ppermute | solution.py:286
  46.6 16.5 %collective-permute-start.11 = (f32[1,512]{1,0:T(1,128)S(1)}, f32[1,512]{1,0:T(1,128)S(1)}, u32[]{:S(2)}, u32[]{:S(2)}) collective-permute-start(f32[1,512]{1,0:T(1,128)S(1)} %slice.22), channel_id=1, source_target_pairs={{0,4},{4,0},{8,12},{12,8},{1,5},{5,1},{9,13},{13,9},{2,6},{6,2},{1... | collective-permute-start | bytes 6152 | tf_op jit(solution)/shard_map/ppermute | solution.py:286
  46.7 1.6 %copy-start.5 = (bf16[1024,1024]{1,0:T(8,128)(2,1)S(1)}, bf16[1024,1024]{1,0:T(8,128)(2,1)}, u32[]{:S(2)}) copy-start(bf16[1024,1024]{1,0:T(8,128)(2,1)} %z_ref.3) | copy-start | bytes 6291460
  49.2 1.6 %copy-start.14 = (bf16[8,128,1024]{2,1,0:T(8,128)(2,1)S(1)}, bf16[8,128,1024]{2,1,0:T(8,128)(2,1)}, u32[]{:S(2)}) copy-start(bf16[8,128,1024]{2,1,0:T(8,128)(2,1)} %copy-done.12) | copy-start | bytes 6291460
  50.8 1.6 %copy-start.17 = (bf16[8,128,1024]{2,1,0:T(8,128)(2,1)S(1)}, bf16[8,128,1024]{2,1,0:T(8,128)(2,1)}, u32[]{:S(2)}) copy-start(bf16[8,128,1024]{2,1,0:T(8,128)(2,1)} %copy-done.15) | copy-start | bytes 6291460
  61.1 15.4 %collective-permute-start.18 = (f32[1,512]{1,0:T(1,128)S(1)}, f32[1,512]{1,0:T(1,128)S(1)}, u32[]{:S(2)}, u32[]{:S(2)}) collective-permute-start(f32[1,512]{1,0:T(1,128)S(1)} %slice.23), channel_id=1, source_target_pairs={{0,8},{4,12},{8,0},{12,4},{1,9},{5,13},{9,1},{13,5},{2,10},{6,14},... | collective-permute-start | bytes 6152 | tf_op jit(solution)/shard_map/ppermute | solution.py:286
  63.1 14.3 %collective-permute-start.19 = (f32[1,512]{1,0:T(1,128)S(1)}, f32[1,512]{1,0:T(1,128)S(1)}, u32[]{:S(2)}, u32[]{:S(2)}) collective-permute-start(f32[1,512]{1,0:T(1,128)S(1)} %slice.23), channel_id=1, source_target_pairs={{0,12},{4,8},{8,4},{12,0},{1,13},{5,9},{9,5},{13,1},{2,14},{6,10},... | collective-permute-start | bytes 6152 | tf_op jit(solution)/shard_map/ppermute | solution.py:286
  64.5 4.2 %collective-permute-start.9 = (bf16[512,512]{1,0:T(8,128)(2,1)}, bf16[512,512]{1,0:T(8,128)(2,1)S(1)}, u32[]{:S(2)}, u32[]{:S(2)}) collective-permute-start(bf16[512,512]{1,0:T(8,128)(2,1)} %collective-permute-done.8), channel_id=1, source_target_pairs={{0,16},{16,0},{1,17},{17,1},{2,18},{18,2},{3,19},{19,3},{4,20},{20... | collective-permute-start | bytes 1572872 | tf_op jit(solution)/shard_map/ppermute | solution.py:186
  64.6 6.9 %collective-permute-start.3 = (bf16[512,512]{1,0:T(8,128)(2,1)}, bf16[512,512]{1,0:T(8,128)(2,1)S(1)}, u32[]{:S(2)}, u32[]{:S(2)}) collective-permute-start(bf16[512,512]{1,0:T(8,128)(2,1)} %collective-permute-done.2), channel_id=1, source_target_pairs={{0,16},{16,0},{1,17},{17,1},{2,18},{18,2},{3,19},{19,3},{4,20},{20... | collective-permute-start | bytes 1572872 | tf_op jit(solution)/shard_map/ppermute | solution.py:186
  65.1 4.4 %collective-permute-start.6 = (bf16[512,512]{1,0:T(8,128)(2,1)}, bf16[512,512]{1,0:T(8,128)(2,1)S(1)}, u32[]{:S(2)}, u32[]{:S(2)}) collective-permute-start(bf16[512,512]{1,0:T(8,128)(2,1)} %collective-permute-done.5), channel_id=1, source_target_pairs={{0,16},{16,0},{1,17},{17,1},{2,18},{18,2},{3,19},{19,3},{4,20},{20... | collective-permute-start | bytes 1572872 | tf_op jit(solution)/shard_map/ppermute | solution.py:186
  72.2 27.7 %collective-permute-start.4 = (bf16[512,512]{1,0:T(8,128)(2,1)S(1)}, bf16[512,512]{1,0:T(8,128)(2,1)S(1)}, u32[]{:S(2)}, u32[]{:S(2)}) collective-permute-start(bf16[512,512]{1,0:T(8,128)(2,1)S(1)} %convolution_convert_fusion.5), channel_id=1, source_target_pairs={{0,4},{4,0},{8,12},{12,8},{1,5},{5,1},{9,13},{13,9},{2,6},{6,2},{1... | collective-permute-start | bytes 1572872 | tf_op jit(solution)/shard_map/ppermute | solution.py:285
  72.4 27.6 %collective-permute-start.7 = (bf16[512,512]{1,0:T(8,128)(2,1)S(1)}, bf16[512,512]{1,0:T(8,128)(2,1)S(1)}, u32[]{:S(2)}, u32[]{:S(2)}) collective-permute-start(bf16[512,512]{1,0:T(8,128)(2,1)S(1)} %convolution_convert_fusion.4), channel_id=1, source_target_pairs={{0,8},{4,12},{8,0},{12,4},{1,9},{5,13},{9,1},{13,5},{2,10},{6,14},... | collective-permute-start | bytes 1572872 | tf_op jit(solution)/shard_map/ppermute | solution.py:285
  74.3 25.7 %collective-permute-start.10 = (bf16[512,512]{1,0:T(8,128)(2,1)S(1)}, bf16[512,512]{1,0:T(8,128)(2,1)S(1)}, u32[]{:S(2)}, u32[]{:S(2)}) collective-permute-start(bf16[512,512]{1,0:T(8,128)(2,1)S(1)} %convolution_convert_fusion.3), channel_id=1, source_target_pairs={{0,12},{4,8},{8,4},{12,0},{1,13},{5,9},{9,5},{13,1},{2,14},{6,10},... | collective-permute-start | bytes 1572872 | tf_op jit(solution)/shard_map/ppermute | solution.py:285
  75.8 24.3 %copy-start.21 = (bf16[4096,512]{1,0:T(8,128)(2,1)S(1)}, bf16[4096,512]{1,0:T(8,128)(2,1)}, u32[]{:S(2)}) copy-start(bf16[4096,512]{1,0:T(8,128)(2,1)} %param.17) | copy-start | bytes 12582916
  76.5 21.9 %collective-permute-start.17 = (f32[1,512]{1,0:T(1,128)S(1)}, f32[1,512]{1,0:T(1,128)S(1)}, u32[]{:S(2)}, u32[]{:S(2)}) collective-permute-start(f32[1,512]{1,0:T(1,128)S(1)} %slice.23), channel_id=1, source_target_pairs={{0,4},{4,0},{8,12},{12,8},{1,5},{5,1},{9,13},{13,9},{2,6},{6,2},{1... | collective-permute-start | bytes 6152 | tf_op jit(solution)/shard_map/ppermute | solution.py:286
  77.4 32.2 %collective-permute-start.14 = (bf16[512,512]{1,0:T(8,128)(2,1)S(1)}, bf16[512,512]{1,0:T(8,128)(2,1)S(1)}, u32[]{:S(2)}, u32[]{:S(2)}) collective-permute-start(bf16[512,512]{1,0:T(8,128)(2,1)S(1)} %convolution_convert_fusion.2), channel_id=1, source_target_pairs={{0,4},{4,0},{8,12},{12,8},{1,5},{5,1},{9,13},{13,9},{2,6},{6,2},{1... | collective-permute-start | bytes 1572872 | tf_op jit(solution)/shard_map/ppermute | solution.py:285
  98.4 24.1 %collective-permute-start.15 = (bf16[512,512]{1,0:T(8,128)(2,1)S(1)}, bf16[512,512]{1,0:T(8,128)(2,1)S(1)}, u32[]{:S(2)}, u32[]{:S(2)}) collective-permute-start(bf16[512,512]{1,0:T(8,128)(2,1)S(1)} %convolution_convert_fusion.1), channel_id=1, source_target_pairs={{0,8},{4,12},{8,0},{12,4},{1,9},{5,13},{9,1},{13,5},{2,10},{6,14},... | collective-permute-start | bytes 1572872 | tf_op jit(solution)/shard_map/ppermute | solution.py:285
  99.9 22.6 %collective-permute-start.16 = (bf16[512,512]{1,0:T(8,128)(2,1)S(1)}, bf16[512,512]{1,0:T(8,128)(2,1)S(1)}, u32[]{:S(2)}, u32[]{:S(2)}) collective-permute-start(bf16[512,512]{1,0:T(8,128)(2,1)S(1)} %convolution_convert_fusion), channel_id=1, source_target_pairs={{0,12},{4,8},{8,4},{12,0},{1,13},{5,9},{9,5},{13,1},{2,14},{6,10},... | collective-permute-start | bytes 1572872 | tf_op jit(solution)/shard_map/ppermute | solution.py:285
  (11 other events, 12.1 us)
where the time goes:
time: 125 us; the launch traced here: 124 us
  waiting for transfers between devices  40.7 us (33%)
  local copies, waits for them, and re-layouts  29.2 us (23%)
  Pallas kernels  24.4 us (20%)
  starting transfers between devices  22.7 us (18%)
  matrix products  5.95 us (5%)
    ppermute x6, waiting for transfers between devices, body(): got.append(lax.ppermute(part, 'chan', perm))  21.6 us
    unnamed x46, local copies, waits for them, and re-layouts  20.8 us
    ppermute x6, waiting for transfers between devices, body(): squares = squares + lax.ppermute(sums, 'chan', perm)  19 us
    pallas_call x2, Pallas kernels, body(): pl.pallas_call(functools.partial(outputs_kernel, heads, width), grid=(cou...  15.3 us
    pallas_call x1, Pallas kernels, body(): pl.pallas_call(functools.partial(states_kernel, heads, width), out_shape=...  9.09 us
    ppermute x6, starting transfers between devices, body(): got.append(lax.ppermute(part, 'chan', perm))  7.1 us
    ppermute x6, starting transfers between devices, body(): squares = squares + lax.ppermute(sums, 'chan', perm)  5.7 us
    ppermute x3, starting transfers between devices, body(): lax.ppermute(part, 'chan', [(i, partner(i, k)) for i in range(n_chan)])  5.31 us
  transfers between devices with their start and end apart: 20, of which 3 were waited for; matrix products, arithmetic and copies ran while one was open for 9% of the time, Pallas kernels for 12%

commit v1 on v0

--- a/solution.py
+++ b/solution.py
@@ -6,6 +6,7 @@
 from jax.experimental import pallas as pl
 from jax.experimental.pallas import tpu as pltpu
 from jax.sharding import PartitionSpec as P
+
 
 Q = 128
 LOG2E = 1.4426950408889634
@@ -79,7 +80,7 @@
         raw = jnp.concatenate(
             [raw_ref[:, pl.ds(at_f, Q)][:heads], raw_ref[:, pl.ds(at_b, Q)][heads:]], axis=0
         )
-        dt, cum, total, rowt = rates_of(raw, hp_ref, heads)
+        _, cum, total, rowt = rates_of(raw, hp_ref, heads)
         gain = jnp.broadcast_to(jnp.exp2(total), cum.shape)
         cols = halves(columns_of([jnp.exp2(total + rowt), gain]))
         for at, block, b_ref, ent, state, dec, place in (
@@ -110,7 +111,7 @@
     def _():
         fill_spread(spread, (2, 3, 5), heads, width)
 
-    dt, cum, total, rowt = rates_of(raw_ref[...], hp_ref, heads)
+    dt, cum, _, rowt = rates_of(raw_ref[...], hp_ref, heads)
     cols = columns_of([cum, jnp.exp2(cum), dt])
     b_f, c_f, b_b, c_b = pf_ref[0], pf_ref[1], pb_ref[0], pb_ref[1]
     lane = lax.broadcasted_iota(jnp.int32, (Q, 128), 1)
@@ -164,20 +165,14 @@
     chan, seq = lax.axis_index("chan"), lax.axis_index("seq")
     all_channels = inner * n_chan
 
-    paired = n_chan & (n_chan - 1) == 0
-
-    def partner(i, k):
-        return i ^ k if paired else (i + k) % n_chan
-
-    def source(i, k):
-        return i ^ k if paired else (i + n_chan - k) % n_chan
+    assert n_chan & (n_chan - 1) == 0
 
     share = inner // n_seq
     pieces = {}
     for k in range(1, n_chan):
-        start = partner(chan, k) * inner + seq * share
+        start = (chan ^ k) * inner + seq * share
         part = lax.dynamic_slice(out_weight, (start, 0), (share, features))
-        pieces[k] = lax.ppermute(part, "chan", [(i, partner(i, k)) for i in range(n_chan)])
+        pieces[k] = lax.ppermute(part, "chan", [(i, i ^ k) for i in range(n_chan)])
     weights = {0: lax.dynamic_slice(out_weight, (chan * inner, 0), (inner, features))}
     for k in range(1, n_chan):
         whole = jnp.zeros((inner, features), out_weight.dtype)
@@ -193,7 +188,7 @@
     skip_row = lax.dynamic_update_slice(skip_row, skip_gain[None], (0, 5 * heads))
     gain_row = norm_gain[None]
 
-    ent_f, ent_b, dec, end_f, end_b, tot = pl.pallas_call(
+    states = pl.pallas_call(
         functools.partial(states_kernel, heads, width),
         out_shape=(
             jax.ShapeDtypeStruct((blocks, state, inner), BF16),
@@ -210,12 +205,15 @@
             pltpu.VMEM((8, inner), F32),
             pltpu.VMEM((4, 256, inner), BF16),
         ],
-        compiler_params=pltpu.CompilerParams(vmem_limit_bytes=40 * 2**20),
+        compiler_params=pltpu.CompilerParams(vmem_limit_bytes=60 * 2**20),
         cost_estimate=pl.CostEstimate(
             flops=4 * 10**9, bytes_accessed=8 * 2**20, transcendentals=0
         ),
         name="scan_states",
-    )(ssm_input, proj_forward[0], proj_backward[0], raw, params)
+    )
+    ent_f, ent_b, dec, end_f, end_b, tot = states(
+        ssm_input, proj_forward[0], proj_backward[0], raw, params
+    )
 
     def carried(end, decay, step):
         pairs = [(i, i + step) for i in range(n_seq) if 0 <= i + step < n_seq]
@@ -230,14 +228,14 @@
 
     chunks = 2 if blocks % 2 == 0 else 1
     count = blocks // chunks
-    received = []
+    owned, squares = [], []
     for chunk in range(chunks):
         at = chunk * count
         rows = lambda i, at=at: (i + at, 0)
         rows3 = lambda i, at=at: (0, i + at, 0)
         block3 = lambda i, at=at: (i + at, 0, 0)
         same = lambda i: (0, 0)
-        gated, sums = pl.pallas_call(
+        outputs = pl.pallas_call(
             functools.partial(outputs_kernel, heads, width),
             grid=(count,),
             in_specs=[
@@ -265,30 +263,39 @@
             ),
             scratch_shapes=[pltpu.VMEM((3, 256, inner), BF16), pltpu.VMEM((Q, inner), F32)],
             compiler_params=pltpu.CompilerParams(
-                vmem_limit_bytes=40 * 2**20, dimension_semantics=("arbitrary",)
+                vmem_limit_bytes=60 * 2**20, dimension_semantics=("arbitrary",)
             ),
             cost_estimate=pl.CostEstimate(
                 flops=4 * 10**9, bytes_accessed=8 * 2**20, transcendentals=0
             ),
             name="scan_outputs",
-        )(
+        )
+        gated, sums = outputs(
             ssm_input, gate_z, proj_forward, proj_backward, raw, params, skip_row, gain_row,
             ent_f, ent_b, dec, carry_f, carry_b,
         )
-        sums = sums[0:1]
-        squares = sums
-        got = []
-        for k in range(1, n_chan):
-            perm = [(i, partner(i, k)) for i in range(n_chan)]
-            kin = k if paired else n_chan - k
-            part = jnp.dot(gated, weights[kin], preferred_element_type=F32).astype(BF16)
-            got.append(lax.ppermute(part, "chan", perm))
-            squares = squares + lax.ppermute(sums, "chan", perm)
-        own = jnp.dot(gated, weights[0], preferred_element_type=F32)
-        for part in got:
-            own = own + part.astype(F32)
-        scale = lax.rsqrt(squares[0] / all_channels + 1.0)
-        received.append((own * scale[:, None]).astype(BF16))
+        bits = [1 << b for b in range(n_chan.bit_length() - 1)]
+        bits = bits if chunk % 2 == 0 else bits[::-1]
+        parts = {
+            r: jnp.dot(gated, weights[r], preferred_element_type=F32)
+            for r in range(n_chan)
+        }
+        for bit in bits:
+            perm = [(i, i ^ bit) for i in range(n_chan)]
+            going = sorted((r for r in parts if r & bit), reverse=True)
+            got = {r ^ bit: lax.ppermute(parts.pop(r).astype(BF16), "chan", perm) for r in going}
+            parts = {r: parts[r] + got[r].astype(F32) for r in parts}
+        owned.append(parts[0])
+        squares.append(sums[0:1])
+    squares = jnp.concatenate(squares, axis=1)
+    for bit in bits:
+        perm = [(i, i ^ bit) for i in range(n_chan)]
+        squares = squares + lax.ppermute(squares, "chan", perm)
+    scale = lax.rsqrt(squares[0] / all_channels + 1.0)[:, None]
+    received = [
+        (part * scale[c * count * Q : (c + 1) * count * Q]).astype(BF16)
+        for c, part in enumerate(owned)
+    ]
     return jnp.concatenate(received, axis=0)
 
 

time: 125 us -> 96.2 us (0.77)
  local copies, waits for them, and re-layouts: 29.2 us -> 9.48 us
  waiting for transfers between devices: 40.7 us -> 30.5 us
  Pallas kernels: 24.4 us -> 29.8 us
  starting transfers between devices: 22.7 us -> 18.8 us
    unnamed x46 -> x10, local copies, waits for them, and re-layouts: 20.8 us -> 1.99 us
    ppermute x15 -> x11, waiting for transfers between devices: 40.7 us -> 30.5 us  [the longest x6 29.5 us: body(): lax.ppermute(parts.pop(r).astype(BF16), 'chan', perm)]
    pallas_call x3, Pallas kernels: 24.4 us -> 29.8 us  [the longest x2 17.7 us: body(): outputs(ssm_input, gate_z, proj_forward, proj_backward, raw, params, skip...]
    ppermute x15 -> x11, starting transfers between devices: 18.1 us -> 13.9 us  [the longest x6 5.99 us: body(): lax.ppermute(parts.pop(r).astype(BF16), 'chan', perm)]
    dynamic_update_slice x3, local copies, waits for them, and re-layouts: 3.25 us -> 0.12 us  [body(): whole = lax.dynamic_update_slice(whole, pieces[k], (seq * share, 0))]
    slice x2 -> x3, local copies, waits for them, and re-layouts: 0.01 us -> 1.44 us  [the longest x2 1.44 us: body(): squares.append(sums[0:1])]
  transfers between devices with their start and end apart: 20 -> 16, of which waited for: 3 -> 6; matrix products, arithmetic and copies ran while one was open for 9% -> 9% of each run, Pallas kernels for 12% -> 18%
where the time goes in v1:
time: 96.2 us; the launch traced here: 95.7 us
  waiting for transfers between devices  30.5 us (32%)
  Pallas kernels  29.8 us (31%)
  starting transfers between devices  18.8 us (20%)
  local copies, waits for them, and re-layouts  9.48 us (10%)
  matrix products  5.78 us (6%)
  other arithmetic  1.08 us (1%)
    ppermute x6, waiting for transfers between devices, body(): lax.ppermute(parts.pop(r).astype(BF16), 'chan', perm)  29.5 us
    pallas_call x2, Pallas kernels, body(): outputs(ssm_input, gate_z, proj_forward, proj_backward, raw, params, skip...  17.7 us
    pallas_call x1, Pallas kernels, body(): states(ssm_input, proj_forward[0], proj_backward[0], raw, params)  12.1 us
    ppermute x6, starting transfers between devices, body(): lax.ppermute(parts.pop(r).astype(BF16), 'chan', perm)  5.99 us
    dot_general x8, matrix products, body(): jnp.dot(gated, weights[r], preferred_element_type=F32)  5.78 us
    ppermute x3, starting transfers between devices, body(): pieces[k] = lax.ppermute(part, 'chan', [(i, i ^ k) for i in range(n_chan)])  3.94 us
    ppermute x2, starting transfers between devices, body(): squares = squares + lax.ppermute(squares, 'chan', perm)  3.94 us
    ppermute x2, starting transfers between devices, carried(): out = lax.ppermute(end, 'seq', pairs)  3.83 us
  transfers between devices with their start and end apart: 16, of which 6 were waited for; matrix products, arithmetic and copies ran while one was open for 9% of the time, Pallas kernels for 18%

profile of v1, /device:TPU:0, one launch (start us, length us, event | category | flops | bytes accessed | tf_op | source)
XLA Modules:
  0.0 95.7 jit_solution(5098684610985242488)
XLA Ops:
  0.0 0.8 slice_reduce_fusion.1
  1.6 1.9 %slice_bitcast_fusion = (bf16[1024,128]{1,0:T(8,128)(2,1)}, bf16[1024,128]{1,0:T(8,128)(2,1)}) fusion(bf16[2,1024,128]{2,1,0:T(8,128)(2,1)} %pb_ref.3, bf16[2,1024,128]{2,1,0:T(8,128)(2,1)} %pf_ref.3), kind=kLoop, calls=%fused_computation.19 | loop fusion | bytes 1048576 | tf_op jit(solution)/shard_map/squeeze | solution.py:215
  3.5 12.1 %scan_states.1 = (bf16[8,128,1024]{2,1,0:T(8,128)(2,1)}, bf16[8,128,1024]{2,1,0:T(8,128)(2,1)}, f32[8,16,1024]{2,1,0:T(8,128)}, bf16[128,1024]{1,0:T(8,128)(2,1)...) custom-call(bf16[1024,1024]{1,0:T(8,128)(2,1)} %x_ref.5, bf16[1024,128]{1,0:T(8,128)(2,1)} %get-tuple-element.31.bf_ref, ...), custom_call_target="tpu_custom_call" | custom-call | flops 4000000000 | bytes 8388608 | tf_op jit(solution)/shard_map/scan_states/pallas_call | solution.py:214
  15.6 2.5 %collective-permute-start = (bf16[128,1024]{1,0:T(8,128)(2,1)}, bf16[128,1024]{1,0:T(8,128)(2,1)S(1)}, u32[]{:S(2)}, u32[]{:S(2)}) collective-permute-start(bf16[128,1024]{1,0:T(8,128)(2,1)} %get-tuple-element.17), channel_id=1, source_target_pairs={{0,16},{1,17},{2,18},{3,19},{4,20},{5,21},{6,22},{7,23},{8,24},{9,... | collective-permute-start | bytes 786440 | tf_op jit(solution)/shard_map/ppermute | solution.py:220
  18.1 1.3 %collective-permute-start.1 = (bf16[128,1024]{1,0:T(8,128)(2,1)}, bf16[128,1024]{1,0:T(8,128)(2,1)}, u32[]{:S(2)}, u32[]{:S(2)}) collective-permute-start(bf16[128,1024]{1,0:T(8,128)(2,1)} %get-tuple-element.18), channel_id=1, source_target_pairs={{16,0},{17,1},{18,2},{19,3},{20,4},{21,5},{22,6},{23,7},{24,8},{25... | collective-permute-start | bytes 786440 | tf_op jit(solution)/shard_map/ppermute | solution.py:220
  19.5 1.5 %constant_dynamic-slice_fusion.1 = (bf16[512,512]{1,0:T(8,128)(2,1)S(1)}, bf16[512,512]{1,0:T(8,128)(2,1)S(1)}, bf16[512,512]{1,0:T(8,128)(2,1)S(1)}) fusion(bf16[4096,512]{1,0:T(8,128)(2,1)} %param.17, s32[]{:T(128)S(6)} %select_n.38, s32[]{:T(128)S(6)} %select_n.34, s32[]{:T(128)S(6)} %select_n.39), kind=kLoop, calls=%fused_computation.29 | loop fusion | bytes 3145740 | tf_op jit(solution)/shard_map/dynamic_slice | solution.py:174
  20.9 2.4 %collective-permute-start.5 = (bf16[512,512]{1,0:T(8,128)(2,1)S(1)}, bf16[512,512]{1,0:T(8,128)(2,1)S(1)}, u32[]{:S(2)}, u32[]{:S(2)}) collective-permute-start(bf16[512,512]{1,0:T(8,128)(2,1)S(1)} %get-tuple-element.25), channel_id=1, source_target_pairs={{0,8},{4,12},{8,0},{12,4},{1,9},{5,13},{9,1},{13,5},{2,10},{6,14},... | collective-permute-start | bytes 1572872 | tf_op jit(solution)/shard_map/ppermute | solution.py:175
  23.3 1.5 %collective-permute-start.2 = (bf16[512,512]{1,0:T(8,128)(2,1)S(1)}, bf16[512,512]{1,0:T(8,128)(2,1)S(1)}, u32[]{:S(2)}, u32[]{:S(2)}) collective-permute-start(bf16[512,512]{1,0:T(8,128)(2,1)S(1)} %get-tuple-element.26), channel_id=1, source_target_pairs={{0,4},{4,0},{8,12},{12,8},{1,5},{5,1},{9,13},{13,9},{2,6},{6,2},{1... | collective-permute-start | bytes 1572872 | tf_op jit(solution)/shard_map/ppermute | solution.py:175
  26.2 8.8 %scan_outputs.3 = (bf16[512,1024]{1,0:T(8,128)(2,1)}, f32[8,512]{1,0:T(8,128)}) custom-call(bf16[1024,1024]{1,0:T(8,128)(2,1)} %x_ref.5, bf16[1024,1024]{1,0:T(8,128)(2,1)} %z_ref.3, bf16[2,1024,128]{2,1,0:T(8,128)(2,1)} %pf_ref.3, bf16[2,1024,128]{2,1,0:T(8,128)(2,1)} %pb_ref.3, f32[32,1024]{1,0:T(8,128)} %bitcast.26, f32[32,2]{1,0:T(8,128)} %copy.15.hp_ref, ...), custom_call_target="tpu_custom_call" | custom-call | flops 4000000000 | bytes 8388608 | tf_op jit(solution)/shard_map/scan_outputs/pallas_call | solution.py:273
  35.1 8.9 %scan_outputs.2 = (bf16[512,1024]{1,0:T(8,128)(2,1)}, f32[8,512]{1,0:T(8,128)}) custom-call(bf16[1024,1024]{1,0:T(8,128)(2,1)} %x_ref.5, bf16[1024,1024]{1,0:T(8,128)(2,1)} %z_ref.3, bf16[2,1024,128]{2,1,0:T(8,128)(2,1)} %pf_ref.3, bf16[2,1024,128]{2,1,0:T(8,128)(2,1)} %pb_ref.3, f32[32,1024]{1,0:T(8,128)} %bitcast.27, f32[32,2]{1,0:T(8,128)} %copy.15.hp_ref, ...), custom_call_target="tpu_custom_call" | custom-call | flops 4000000000 | bytes 8388608 | tf_op jit(solution)/shard_map/scan_outputs/pallas_call | solution.py:273
  43.9 0.7 slice.36
  44.6 0.7 slice.37
  45.4 1.9 %collective-permute-start.11 = (f32[1,1024]{1,0:T(1,128)S(1)}, f32[1,1024]{1,0:T(1,128)S(1)}, u32[]{:S(2)}, u32[]{:S(2)}) collective-permute-start(f32[1,1024]{1,0:T(1,128)S(1)} %pad_maximum_fusion.1), channel_id=1, source_target_pairs={{0,8},{4,12},{8,0},{12,4},{1,9},{5,13},{9,1},{13,5},{2,10},{6,14},... | collective-permute-start | bytes 12296 | tf_op jit(solution)/shard_map/ppermute | solution.py:293
  47.3 0.8 collective-permute-done.7
  49.0 2.0 %collective-permute-start.12 = (f32[1,1024]{1,0:T(1,128)S(1)}, f32[1,1024]{1,0:T(1,128)S(1)}, u32[]{:S(2)}, u32[]{:S(2)}) collective-permute-start(f32[1,1024]{1,0:T(1,128)S(1)} %fusion.12), channel_id=1, source_target_pairs={{0,4},{4,0},{8,12},{12,8},{1,5},{5,1},{9,13},{13,9},{2,6},{6,2},{1... | collective-permute-start | bytes 12296 | tf_op jit(solution)/shard_map/ppermute | solution.py:293
  51.9 1.0 %copy-done.4 = bf16[512,1024]{1,0:T(8,128)(2,1)S(1)} copy-done((bf16[512,1024]{1,0:T(8,128)(2,1)S(1)}, bf16[512,1024]{1,0:T(8,128)(2,1)}, u32[]{:S(2)}) %copy-start.4) | copy-done | bytes 1048600
  52.9 0.7 convolution_convert_fusion.2
  54.1 0.7 convolution_convert_fusion
  54.9 0.7 convolution_convert_fusion.3
  55.6 1.7 %collective-permute-start.4 = (bf16[512,512]{1,0:T(8,128)(2,1)S(1)}, bf16[512,512]{1,0:T(8,128)(2,1)S(1)}, u32[]{:S(2)}, u32[]{:S(2)}) collective-permute-start(bf16[512,512]{1,0:T(8,128)(2,1)S(1)} %convolution_convert_fusion.3), channel_id=1, source_target_pairs={{0,4},{4,0},{8,12},{12,8},{1,5},{5,1},{9,13},{13,9},{2,6},{6,2},{1... | collective-permute-start | bytes 1572872 | tf_op jit(solution)/shard_map/ppermute | solution.py:286
  57.3 1.5 %collective-permute-start.14 = (bf16[512,512]{1,0:T(8,128)(2,1)S(1)}, bf16[512,512]{1,0:T(8,128)(2,1)S(1)}, u32[]{:S(2)}, u32[]{:S(2)}) collective-permute-start(bf16[512,512]{1,0:T(8,128)(2,1)S(1)} %convolution_convert_fusion), channel_id=1, source_target_pairs={{0,8},{4,12},{8,0},{12,4},{1,9},{5,13},{9,1},{13,5},{2,10},{6,14},... | collective-permute-start | bytes 1572872 | tf_op jit(solution)/shard_map/ppermute | solution.py:286
  58.8 0.7 convolution_convert_fusion.1
  60.1 8.4 %collective-permute-done.9 = bf16[512,512]{1,0:T(8,128)(2,1)S(1)} collective-permute-done((bf16[512,512]{1,0:T(8,128)(2,1)S(1)}, bf16[512,512]{1,0:T(8,128)(2,1)S(1)}, u32[]{:S(2)}, u32[]{:S(2)}) %collective-permute-start.9) | collective-permute-done | bytes 524320 | tf_op jit(solution)/shard_map/ppermute | solution.py:286
  68.5 0.7 fusion.4
  69.2 1.6 %collective-permute-start.10 = (bf16[512,512]{1,0:T(8,128)(2,1)S(1)}, bf16[512,512]{1,0:T(8,128)(2,1)S(1)}, u32[]{:S(2)}, u32[]{:S(2)}) collective-permute-start(bf16[512,512]{1,0:T(8,128)(2,1)S(1)} %fusion.4), channel_id=1, source_target_pairs={{0,8},{4,12},{8,0},{12,4},{1,9},{5,13},{9,1},{13,5},{2,10},{6,14},... | collective-permute-start | bytes 1572872 | tf_op jit(solution)/shard_map/ppermute | solution.py:286
  70.8 1.3 %collective-permute-done.14 = bf16[512,512]{1,0:T(8,128)(2,1)S(1)} collective-permute-done((bf16[512,512]{1,0:T(8,128)(2,1)S(1)}, bf16[512,512]{1,0:T(8,128)(2,1)S(1)}, u32[]{:S(2)}, u32[]{:S(2)}) %collective-permute-start.14) | collective-permute-done | bytes 524320 | tf_op jit(solution)/shard_map/ppermute | solution.py:286
  72.1 0.7 fusion.5
  73.3 6.5 %collective-permute-done.4 = bf16[512,512]{1,0:T(8,128)(2,1)S(1)} collective-permute-done((bf16[512,512]{1,0:T(8,128)(2,1)S(1)}, bf16[512,512]{1,0:T(8,128)(2,1)S(1)}, u32[]{:S(2)}, u32[]{:S(2)}) %collective-permute-start.4) | collective-permute-done | bytes 524320 | tf_op jit(solution)/shard_map/ppermute | solution.py:286
  79.7 13.3 %collective-permute-done.10 = bf16[512,512]{1,0:T(8,128)(2,1)S(1)} collective-permute-done((bf16[512,512]{1,0:T(8,128)(2,1)S(1)}, bf16[512,512]{1,0:T(8,128)(2,1)S(1)}, u32[]{:S(2)}, u32[]{:S(2)}) %collective-permute-start.10) | collective-permute-done | bytes 524320 | tf_op jit(solution)/shard_map/ppermute | solution.py:286
  93.1 0.8 fusion.7
  93.9 0.8 fusion.6
  94.7 1.0 %pad_maximum_fusion = bf16[1024,512]{1,0:T(8,128)(2,1)} fusion(bf16[512,512]{1,0:T(8,128)(2,1)S(1)} %fusion.6, bf16[512,512]{1,0:T(8,128)(2,1)S(1)} %fusion.7), kind=kLoop, calls=%fused_computation.16 | loop fusion | flops 2097152 | bytes 2097152 | tf_op jit(solution)/shard_map/concatenate | solution.py:299
  (45 shorter events, 5.7 us)
Async XLA Ops:
  15.6 9.3 %copy-start.2 = (f32[16]{0:T(128)S(1)}, f32[16]{0:T(128)}, u32[]{:S(2)}) copy-start(f32[16]{0:T(128)} %param.15) | copy-start | bytes 196
  15.6 9.9 %collective-permute-start = (bf16[128,1024]{1,0:T(8,128)(2,1)}, bf16[128,1024]{1,0:T(8,128)(2,1)S(1)}, u32[]{:S(2)}, u32[]{:S(2)}) collective-permute-start(bf16[128,1024]{1,0:T(8,128)(2,1)} %get-tuple-element.17), channel_id=1, source_target_pairs={{0,16},{1,17},{2,18},{3,19},{4,20},{5,21},{6,22},{7,23},{8,24},{9,... | collective-permute-start | bytes 786440 | tf_op jit(solution)/shard_map/ppermute | solution.py:220
  18.1 7.4 %collective-permute-start.1 = (bf16[128,1024]{1,0:T(8,128)(2,1)}, bf16[128,1024]{1,0:T(8,128)(2,1)}, u32[]{:S(2)}, u32[]{:S(2)}) collective-permute-start(bf16[128,1024]{1,0:T(8,128)(2,1)} %get-tuple-element.18), channel_id=1, source_target_pairs={{16,0},{17,1},{18,2},{19,3},{20,4},{21,5},{22,6},{23,7},{24,8},{25... | collective-permute-start | bytes 786440 | tf_op jit(solution)/shard_map/ppermute | solution.py:220
  20.9 30.0 %collective-permute-start.5 = (bf16[512,512]{1,0:T(8,128)(2,1)S(1)}, bf16[512,512]{1,0:T(8,128)(2,1)S(1)}, u32[]{:S(2)}, u32[]{:S(2)}) collective-permute-start(bf16[512,512]{1,0:T(8,128)(2,1)S(1)} %get-tuple-element.25), channel_id=1, source_target_pairs={{0,8},{4,12},{8,0},{12,4},{1,9},{5,13},{9,1},{13,5},{2,10},{6,14},... | collective-permute-start | bytes 1572872 | tf_op jit(solution)/shard_map/ppermute | solution.py:175
  23.3 27.6 %collective-permute-start.2 = (bf16[512,512]{1,0:T(8,128)(2,1)S(1)}, bf16[512,512]{1,0:T(8,128)(2,1)S(1)}, u32[]{:S(2)}, u32[]{:S(2)}) collective-permute-start(bf16[512,512]{1,0:T(8,128)(2,1)S(1)} %get-tuple-element.26), channel_id=1, source_target_pairs={{0,4},{4,0},{8,12},{12,8},{1,5},{5,1},{9,13},{13,9},{2,6},{6,2},{1... | collective-permute-start | bytes 1572872 | tf_op jit(solution)/shard_map/ppermute | solution.py:175
  24.8 23.2 %collective-permute-start.7 = (bf16[512,512]{1,0:T(8,128)(2,1)S(1)}, bf16[512,512]{1,0:T(8,128)(2,1)S(1)}, u32[]{:S(2)}, u32[]{:S(2)}) collective-permute-start(bf16[512,512]{1,0:T(8,128)(2,1)S(1)} %get-tuple-element.27), channel_id=1, source_target_pairs={{0,12},{4,8},{8,4},{12,0},{1,13},{5,9},{9,5},{13,1},{2,14},{6,10},... | collective-permute-start | bytes 1572872 | tf_op jit(solution)/shard_map/ppermute | solution.py:175
  25.5 0.7 copy-start.1
  45.4 3.6 %collective-permute-start.11 = (f32[1,1024]{1,0:T(1,128)S(1)}, f32[1,1024]{1,0:T(1,128)S(1)}, u32[]{:S(2)}, u32[]{:S(2)}) collective-permute-start(f32[1,1024]{1,0:T(1,128)S(1)} %pad_maximum_fusion.1), channel_id=1, source_target_pairs={{0,8},{4,12},{8,0},{12,4},{1,9},{5,13},{9,1},{13,5},{2,10},{6,14},... | collective-permute-start | bytes 12296 | tf_op jit(solution)/shard_map/ppermute | solution.py:293
  48.1 3.8 %collective-permute-start.8 = (bf16[512,512]{1,0:T(8,128)(2,1)S(1)}, bf16[512,512]{1,0:T(8,128)(2,1)S(1)}, u32[]{:S(2)}, u32[]{:S(2)}) collective-permute-start(bf16[512,512]{1,0:T(8,128)(2,1)S(1)} %collective-permute-done.7), channel_id=1, source_target_pairs={{0,16},{16,0},{1,17},{17,1},{2,18},{18,2},{3,19},{19,3},{4,20},{20... | collective-permute-start | bytes 1572872 | tf_op jit(solution)/shard_map/ppermute | solution.py:181
  49.0 24.3 %collective-permute-start.12 = (f32[1,1024]{1,0:T(1,128)S(1)}, f32[1,1024]{1,0:T(1,128)S(1)}, u32[]{:S(2)}, u32[]{:S(2)}) collective-permute-start(f32[1,1024]{1,0:T(1,128)S(1)} %fusion.12), channel_id=1, source_target_pairs={{0,4},{4,0},{8,12},{12,8},{1,5},{5,1},{9,13},{13,9},{2,6},{6,2},{1... | collective-permute-start | bytes 12296 | tf_op jit(solution)/shard_map/ppermute | solution.py:293
  51.0 7.8 %collective-permute-start.6 = (bf16[512,512]{1,0:T(8,128)(2,1)S(1)}, bf16[512,512]{1,0:T(8,128)(2,1)S(1)}, u32[]{:S(2)}, u32[]{:S(2)}) collective-permute-start(bf16[512,512]{1,0:T(8,128)(2,1)S(1)} %collective-permute-done.5), channel_id=1, source_target_pairs={{0,16},{16,0},{1,17},{17,1},{2,18},{18,2},{3,19},{19,3},{4,20},{20... | collective-permute-start | bytes 1572872 | tf_op jit(solution)/shard_map/ppermute | solution.py:181
  51.0 2.8 %collective-permute-start.3 = (bf16[512,512]{1,0:T(8,128)(2,1)S(1)}, bf16[512,512]{1,0:T(8,128)(2,1)S(1)}, u32[]{:S(2)}, u32[]{:S(2)}) collective-permute-start(bf16[512,512]{1,0:T(8,128)(2,1)S(1)} %collective-permute-done.2), channel_id=1, source_target_pairs={{0,16},{16,0},{1,17},{17,1},{2,18},{18,2},{3,19},{19,3},{4,20},{20... | collective-permute-start | bytes 1572872 | tf_op jit(solution)/shard_map/ppermute | solution.py:181
  51.7 1.2 %copy-start.4 = (bf16[512,1024]{1,0:T(8,128)(2,1)S(1)}, bf16[512,1024]{1,0:T(8,128)(2,1)}, u32[]{:S(2)}) copy-start(bf16[512,1024]{1,0:T(8,128)(2,1)} %get-tuple-element.19) | copy-start | bytes 3145732
  52.9 1.2 %copy-start.3 = (bf16[512,1024]{1,0:T(8,128)(2,1)S(1)}, bf16[512,1024]{1,0:T(8,128)(2,1)}, u32[]{:S(2)}) copy-start(bf16[512,1024]{1,0:T(8,128)(2,1)} %get-tuple-element.22) | copy-start | bytes 3145732
  53.6 14.9 %collective-permute-start.9 = (bf16[512,512]{1,0:T(8,128)(2,1)S(1)}, bf16[512,512]{1,0:T(8,128)(2,1)S(1)}, u32[]{:S(2)}, u32[]{:S(2)}) collective-permute-start(bf16[512,512]{1,0:T(8,128)(2,1)S(1)} %convolution_convert_fusion.2), channel_id=1, source_target_pairs={{0,4},{4,0},{8,12},{12,8},{1,5},{5,1},{9,13},{13,9},{2,6},{6,2},{1... | collective-permute-start | bytes 1572872 | tf_op jit(solution)/shard_map/ppermute | solution.py:286
  55.6 24.2 %collective-permute-start.4 = (bf16[512,512]{1,0:T(8,128)(2,1)S(1)}, bf16[512,512]{1,0:T(8,128)(2,1)S(1)}, u32[]{:S(2)}, u32[]{:S(2)}) collective-permute-start(bf16[512,512]{1,0:T(8,128)(2,1)S(1)} %convolution_convert_fusion.3), channel_id=1, source_target_pairs={{0,4},{4,0},{8,12},{12,8},{1,5},{5,1},{9,13},{13,9},{2,6},{6,2},{1... | collective-permute-start | bytes 1572872 | tf_op jit(solution)/shard_map/ppermute | solution.py:286
  57.3 14.8 %collective-permute-start.14 = (bf16[512,512]{1,0:T(8,128)(2,1)S(1)}, bf16[512,512]{1,0:T(8,128)(2,1)S(1)}, u32[]{:S(2)}, u32[]{:S(2)}) collective-permute-start(bf16[512,512]{1,0:T(8,128)(2,1)S(1)} %convolution_convert_fusion), channel_id=1, source_target_pairs={{0,8},{4,12},{8,0},{12,4},{1,9},{5,13},{9,1},{13,5},{2,10},{6,14},... | collective-permute-start | bytes 1572872 | tf_op jit(solution)/shard_map/ppermute | solution.py:286
  59.5 34.3 %collective-permute-start.13 = (bf16[512,512]{1,0:T(8,128)(2,1)S(1)}, bf16[512,512]{1,0:T(8,128)(2,1)S(1)}, u32[]{:S(2)}, u32[]{:S(2)}) collective-permute-start(bf16[512,512]{1,0:T(8,128)(2,1)S(1)} %convolution_convert_fusion.1), channel_id=1, source_target_pairs={{0,8},{4,12},{8,0},{12,4},{1,9},{5,13},{9,1},{13,5},{2,10},{6,14},... | collective-permute-start | bytes 1572872 | tf_op jit(solution)/shard_map/ppermute | solution.py:286
  68.5 24.6 %copy-start = (bf16[4096,512]{1,0:T(8,128)(2,1)S(1)}, bf16[4096,512]{1,0:T(8,128)(2,1)}, u32[]{:S(2)}) copy-start(bf16[4096,512]{1,0:T(8,128)(2,1)} %param.17) | copy-start | bytes 12582916
  69.2 23.9 %collective-permute-start.10 = (bf16[512,512]{1,0:T(8,128)(2,1)S(1)}, bf16[512,512]{1,0:T(8,128)(2,1)S(1)}, u32[]{:S(2)}, u32[]{:S(2)}) collective-permute-start(bf16[512,512]{1,0:T(8,128)(2,1)S(1)} %fusion.4), channel_id=1, source_target_pairs={{0,8},{4,12},{8,0},{12,4},{1,9},{5,13},{9,1},{13,5},{2,10},{6,14},... | collective-permute-start | bytes 1572872 | tf_op jit(solution)/shard_map/ppermute | solution.py:286
  72.8 21.1 %collective-permute-start.15 = (bf16[512,512]{1,0:T(8,128)(2,1)S(1)}, bf16[512,512]{1,0:T(8,128)(2,1)S(1)}, u32[]{:S(2)}, u32[]{:S(2)}) collective-permute-start(bf16[512,512]{1,0:T(8,128)(2,1)S(1)} %fusion.5), channel_id=1, source_target_pairs={{0,4},{4,0},{8,12},{12,8},{1,5},{5,1},{9,13},{13,9},{2,6},{6,2},{1... | collective-permute-start | bytes 1572872 | tf_op jit(solution)/shard_map/ppermute | solution.py:286

commit v2 on v1

--- a/solution.py
+++ b/solution.py
@@ -173,14 +173,25 @@
         start = (chan ^ k) * inner + seq * share
         part = lax.dynamic_slice(out_weight, (start, 0), (share, features))
         pieces[k] = lax.ppermute(part, "chan", [(i, i ^ k) for i in range(n_chan)])
-    weights = {0: lax.dynamic_slice(out_weight, (chan * inner, 0), (inner, features))}
+    own_weight = lax.dynamic_slice(out_weight, (chan * inner, 0), (inner, features))
+    weights = {}
     for k in range(1, n_chan):
-        whole = jnp.zeros((inner, features), out_weight.dtype)
-        whole = lax.dynamic_update_slice(whole, pieces[k], (seq * share, 0))
+        weights[k] = [(seq * share, pieces[k])]
         for j in range(1, n_seq):
             got = lax.ppermute(pieces[k], "seq", [(i, (i + j) % n_seq) for i in range(n_seq)])
-            whole = lax.dynamic_update_slice(whole, got, (((seq + n_seq - j) % n_seq) * share, 0))
-        weights[k] = whole
+            weights[k].append((((seq + n_seq - j) % n_seq) * share, got))
+
+    def product(gated, k):
+        if k == 0:
+            return jnp.dot(gated, own_weight, preferred_element_type=F32)
+        return sum(
+            jnp.dot(
+                lax.dynamic_slice(gated, (0, at), (gated.shape[0], share)),
+                part,
+                preferred_element_type=F32,
+            )
+            for at, part in weights[k]
+        )
 
     raw = step_raw.reshape(2 * heads, frames)
     params = jnp.stack([head_params[:, 0].reshape(-1), head_params[:, 1].reshape(-1)], axis=1)
@@ -226,7 +237,7 @@
     carry_f = carried(end_f, tot[0:1], 1)
     carry_b = carried(end_b, tot[8:9], -1)
 
-    chunks = 2 if blocks % 2 == 0 else 1
+    chunks = next(c for c in (4, 2, 1) if blocks % c == 0)
     count = blocks // chunks
     owned, squares = [], []
     for chunk in range(chunks):
@@ -276,15 +287,14 @@
         )
         bits = [1 << b for b in range(n_chan.bit_length() - 1)]
         bits = bits if chunk % 2 == 0 else bits[::-1]
-        parts = {
-            r: jnp.dot(gated, weights[r], preferred_element_type=F32)
-            for r in range(n_chan)
-        }
+        parts = {r: product(gated, r) for r in range(n_chan)}
         for bit in bits:
             perm = [(i, i ^ bit) for i in range(n_chan)]
-            going = sorted((r for r in parts if r & bit), reverse=True)
-            got = {r ^ bit: lax.ppermute(parts.pop(r).astype(BF16), "chan", perm) for r in going}
-            parts = {r: parts[r] + got[r].astype(F32) for r in parts}
+            going = [r for r in parts if r & bit]
+            got = jnp.concatenate([parts.pop(r).astype(BF16) for r in going], axis=0)
+            got = lax.ppermute(got, "chan", perm)
+            for r, part in zip(going, jnp.split(got, len(going), axis=0)):
+                parts[r ^ bit] = parts[r ^ bit] + part.astype(F32)
         owned.append(parts[0])
         squares.append(sums[0:1])
     squares = jnp.concatenate(squares, axis=1)

time: 96.2 us -> 124 us (1.29)
  waiting for transfers between devices: 30.5 us -> 47.1 us
  Pallas kernels: 29.8 us -> 34 us
  matrix products: 5.78 us -> 9.02 us
  starting transfers between devices: 18.8 us -> 21 us
    ppermute x2, waiting for transfers between devices: 0.26 us -> 20.2 us  [body(): squares = squares + lax.ppermute(squares, 'chan', perm)]
    ppermute x6 -> x8, waiting for transfers between devices: 29.5 us -> 24.2 us  [body(): got = lax.ppermute(got, 'chan', perm)]
    pallas_call x2 -> x4, Pallas kernels: 17.7 us -> 22 us  [body(): outputs(ssm_input, gate_z, proj_forward, proj_backward, raw, params, skip...]
    ppermute x6 -> x8, starting transfers between devices: 5.99 us -> 9.33 us  [body(): got = lax.ppermute(got, 'chan', perm)]
    dot_general x8 -> x28, matrix products: 5.78 us -> 9.02 us  [the longest x24 7.14 us: product(): jnp.dot(lax.dynamic_slice(gated, (0, at), (gated.shape[0], share)), part,...]
    ppermute x2, waiting for transfers between devices: 0.01 us -> 1.63 us  [carried(): out = lax.ppermute(end, 'seq', pairs)]
    slice x2 -> x4, local copies, waits for them, and re-layouts: 1.44 us -> 2.85 us  [body(): squares.append(sums[0:1])]
  transfers between devices with their start and end apart: 16 -> 18, of which waited for: 6 -> 7; matrix products, arithmetic and copies ran while one was open for 9% -> 10% of each run, Pallas kernels for 18% -> 0%
where the time goes in v2:
time: 124 us; the launch traced here: 123 us
  waiting for transfers between devices  47.1 us (38%)
  Pallas kernels  34 us (27%)
  starting transfers between devices  21 us (17%)
  local copies, waits for them, and re-layouts  10.3 us (8%)
  matrix products  9.02 us (7%)
    ppermute x8, waiting for transfers between devices, body(): got = lax.ppermute(got, 'chan', perm)  24.2 us
    pallas_call x4, Pallas kernels, body(): outputs(ssm_input, gate_z, proj_forward, proj_backward, raw, params, skip...  22 us
    ppermute x2, waiting for transfers between devices, body(): squares = squares + lax.ppermute(squares, 'chan', perm)  20.2 us
    pallas_call x1, Pallas kernels, body(): states(ssm_input, proj_forward[0], proj_backward[0], raw, params)  12.1 us
    ppermute x8, starting transfers between devices, body(): got = lax.ppermute(got, 'chan', perm)  9.33 us
    dot_general x24, matrix products, product(): jnp.dot(lax.dynamic_slice(gated, (0, at), (gated.shape[0], share)), part,...  7.14 us
    ppermute x2, starting transfers between devices, body(): squares = squares + lax.ppermute(squares, 'chan', perm)  4.37 us
    ppermute x2, starting transfers between devices, carried(): out = lax.ppermute(end, 'seq', pairs)  3.69 us
  transfers between devices with their start and end apart: 18, of which 7 were waited for; matrix products, arithmetic and copies ran while one was open for 10% of the time, Pallas kernels for 0%

profile of v2, /device:TPU:0, one launch (start us, length us, event | category | flops | bytes accessed | tf_op | source)
XLA Modules:
  0.0 123.2 jit_solution(3185369559073793568)
XLA Ops:
  0.0 0.8 slice_reduce_fusion.1
  1.6 1.9 %slice_bitcast_fusion = (bf16[1024,128]{1,0:T(8,128)(2,1)}, bf16[1024,128]{1,0:T(8,128)(2,1)}) fusion(bf16[2,1024,128]{2,1,0:T(8,128)(2,1)} %pb_ref.7, bf16[2,1024,128]{2,1,0:T(8,128)(2,1)} %pf_ref.7), kind=kLoop, calls=%fused_computation.53 | loop fusion | bytes 1048576 | tf_op jit(solution)/shard_map/squeeze | solution.py:226
  3.5 12.1 %scan_states.1 = (bf16[8,128,1024]{2,1,0:T(8,128)(2,1)}, bf16[8,128,1024]{2,1,0:T(8,128)(2,1)}, f32[8,16,1024]{2,1,0:T(8,128)}, bf16[128,1024]{1,0:T(8,128)(2,1)...) custom-call(bf16[1024,1024]{1,0:T(8,128)(2,1)} %x_ref.9, bf16[1024,128]{1,0:T(8,128)(2,1)} %get-tuple-element.41.bf_ref, ...), custom_call_target="tpu_custom_call" | custom-call | flops 4000000000 | bytes 8388608 | tf_op jit(solution)/shard_map/scan_states/pallas_call | solution.py:225
  15.6 2.4 %collective-permute-start = (bf16[128,1024]{1,0:T(8,128)(2,1)}, bf16[128,1024]{1,0:T(8,128)(2,1)S(1)}, u32[]{:S(2)}, u32[]{:S(2)}) collective-permute-start(bf16[128,1024]{1,0:T(8,128)(2,1)} %get-tuple-element.21), channel_id=1, source_target_pairs={{0,16},{1,17},{2,18},{3,19},{4,20},{5,21},{6,22},{7,23},{8,24},{9,... | collective-permute-start | bytes 786440 | tf_op jit(solution)/shard_map/ppermute | solution.py:231
  18.0 1.3 %collective-permute-start.1 = (bf16[128,1024]{1,0:T(8,128)(2,1)}, bf16[128,1024]{1,0:T(8,128)(2,1)S(1)}, u32[]{:S(2)}, u32[]{:S(2)}) collective-permute-start(bf16[128,1024]{1,0:T(8,128)(2,1)} %get-tuple-element.22), channel_id=1, source_target_pairs={{16,0},{17,1},{18,2},{19,3},{20,4},{21,5},{22,6},{23,7},{24,8},{25... | collective-permute-start | bytes 786440 | tf_op jit(solution)/shard_map/ppermute | solution.py:231
  20.0 1.6 %collective-permute-done.1.cb_ref = bf16[128,1024]{1,0:T(8,128)(2,1)S(1)} collective-permute-done((bf16[128,1024]{1,0:T(8,128)(2,1)}, bf16[128,1024]{1,0:T(8,128)(2,1)S(1)}, u32[]{:S(2)}, u32[]{:S(2)}) %collective-permute-start.1) | collective-permute-done | bytes 262176 | tf_op jit(solution)/shard_map/ppermute | solution.py:231
  21.6 0.7 copy-done.6
  22.3 5.5 %scan_outputs.4 = (bf16[256,1024]{1,0:T(8,128)(2,1)}, f32[8,256]{1,0:T(8,128)}) custom-call(bf16[1024,1024]{1,0:T(8,128)(2,1)} %x_ref.9, bf16[1024,1024]{1,0:T(8,128)(2,1)} %z_ref.7, bf16[2,1024,128]{2,1,0:T(8,128)(2,1)} %pf_ref.7, bf16[2,1024,128]{2,1,0:T(8,128)(2,1)} %pb_ref.7, f32[32,1024]{1,0:T(8,128)} %bitcast.44, f32[32,2]{1,0:T(8,128)} %copy.15.hp_ref, ...), custom_call_target="tpu_custom_call" | custom-call | flops 4000000000 | bytes 8388608 | tf_op jit(solution)/shard_map/scan_outputs/pallas_call | solution.py:284
  28.5 5.5 %scan_outputs.5 = (bf16[256,1024]{1,0:T(8,128)(2,1)}, f32[8,256]{1,0:T(8,128)}) custom-call(bf16[1024,1024]{1,0:T(8,128)(2,1)} %x_ref.9, bf16[1024,1024]{1,0:T(8,128)(2,1)} %z_ref.7, bf16[2,1024,128]{2,1,0:T(8,128)(2,1)} %pf_ref.7, bf16[2,1024,128]{2,1,0:T(8,128)(2,1)} %pb_ref.7, f32[32,1024]{1,0:T(8,128)} %bitcast.45, f32[32,2]{1,0:T(8,128)} %copy.15.hp_ref, ...), custom_call_target="tpu_custom_call" | custom-call | flops 4000000000 | bytes 8388608 | tf_op jit(solution)/shard_map/scan_outputs/pallas_call | solution.py:284
  34.0 0.7 slice.57
  34.7 5.5 %scan_outputs.6 = (bf16[256,1024]{1,0:T(8,128)(2,1)}, f32[8,256]{1,0:T(8,128)}) custom-call(bf16[1024,1024]{1,0:T(8,128)(2,1)} %x_ref.9, bf16[1024,1024]{1,0:T(8,128)(2,1)} %z_ref.7, bf16[2,1024,128]{2,1,0:T(8,128)(2,1)} %pf_ref.7, bf16[2,1024,128]{2,1,0:T(8,128)(2,1)} %pb_ref.7, f32[32,1024]{1,0:T(8,128)} %bitcast.46, f32[32,2]{1,0:T(8,128)} %copy.15.hp_ref, ...), custom_call_target="tpu_custom_call" | custom-call | flops 4000000000 | bytes 8388608 | tf_op jit(solution)/shard_map/scan_outputs/pallas_call | solution.py:284
  40.2 0.7 slice.58
  40.9 5.5 %scan_outputs.7 = (bf16[256,1024]{1,0:T(8,128)(2,1)}, f32[8,256]{1,0:T(8,128)}) custom-call(bf16[1024,1024]{1,0:T(8,128)(2,1)} %x_ref.9, bf16[1024,1024]{1,0:T(8,128)(2,1)} %z_ref.7, bf16[2,1024,128]{2,1,0:T(8,128)(2,1)} %pf_ref.7, bf16[2,1024,128]{2,1,0:T(8,128)(2,1)} %pb_ref.7, f32[32,1024]{1,0:T(8,128)} %bitcast.47, f32[32,2]{1,0:T(8,128)} %copy.15.hp_ref, ...), custom_call_target="tpu_custom_call" | custom-call | flops 4000000000 | bytes 8388608 | tf_op jit(solution)/shard_map/scan_outputs/pallas_call | solution.py:284
  46.4 0.8 slice.59
  47.2 2.3 %collective-permute-start.10 = (f32[1,1024]{1,0:T(1,128)S(1)}, f32[1,1024]{1,0:T(1,128)S(1)}, u32[]{:S(2)}, u32[]{:S(2)}) collective-permute-start(f32[1,1024]{1,0:T(1,128)S(1)} %pad_maximum_fusion.5), channel_id=1, source_target_pairs={{0,8},{4,12},{8,0},{12,4},{1,9},{5,13},{9,1},{13,5},{2,10},{6,14},... | collective-permute-start | bytes 12296 | tf_op jit(solution)/shard_map/ppermute | solution.py:303
  49.5 2.4 %constant_dynamic-slice_fusion = (bf16[512,512]{1,0:T(8,128)(2,1)S(1)}, bf16[512,512]{1,0:T(8,128)(2,1)}, bf16[512,512]{1,0:T(8,128)(2,1)}) fusion(bf16[4096,512]{1,0:T(8,128)(2,1)} %param.17, s32[]{:T(128)S(6)} %select_n.29, s32[]{:T(128)S(6)} %select_n.25, s32[]{:T(128)S(6)} %select_n.28), kind=kLoop, calls=%fused_computation.118 | loop fusion | bytes 3145740 | tf_op jit(solution)/shard_map/dynamic_slice | solution.py:174
  51.9 1.5 %collective-permute-start.2 = (bf16[512,512]{1,0:T(8,128)(2,1)}, bf16[512,512]{1,0:T(8,128)(2,1)S(1)}, u32[]{:S(2)}, u32[]{:S(2)}) collective-permute-start(bf16[512,512]{1,0:T(8,128)(2,1)} %get-tuple-element.34), channel_id=1, source_target_pairs={{0,4},{4,0},{8,12},{12,8},{1,5},{5,1},{9,13},{13,9},{2,6},{6,2},{1... | collective-permute-start | bytes 1572872 | tf_op jit(solution)/shard_map/ppermute | solution.py:175
  53.4 2.0 %collective-permute-start.11 = (f32[1,1024]{1,0:T(1,128)S(1)}, f32[1,1024]{1,0:T(1,128)S(1)}, u32[]{:S(2)}, u32[]{:S(2)}) collective-permute-start(f32[1,1024]{1,0:T(1,128)S(1)} %fusion.125), channel_id=1, source_target_pairs={{0,4},{4,0},{8,12},{12,8},{1,5},{5,1},{9,13},{13,9},{2,6},{6,2},{1... | collective-permute-start | bytes 12296 | tf_op jit(solution)/shard_map/ppermute | solution.py:303
  55.5 1.5 %collective-permute-start.7 = (bf16[512,512]{1,0:T(8,128)(2,1)S(1)}, bf16[512,512]{1,0:T(8,128)(2,1)S(1)}, u32[]{:S(2)}, u32[]{:S(2)}) collective-permute-start(bf16[512,512]{1,0:T(8,128)(2,1)S(1)} %get-tuple-element.33), channel_id=1, source_target_pairs={{0,8},{4,12},{8,0},{12,4},{1,9},{5,13},{9,1},{13,5},{2,10},{6,14},... | collective-permute-start | bytes 1572872 | tf_op jit(solution)/shard_map/ppermute | solution.py:175
  57.0 20.2 %collective-permute-done.11 = f32[1,1024]{1,0:T(1,128)S(1)} collective-permute-done((f32[1,1024]{1,0:T(1,128)S(1)}, f32[1,1024]{1,0:T(1,128)S(1)}, u32[]{:S(2)}, u32[]{:S(2)}) %collective-permute-start.11) | collective-permute-done | bytes 4128 | tf_op jit(solution)/shard_map/ppermute | solution.py:303
  78.4 1.1 collective-permute-done.7
  84.7 1.7 %collective-permute-start.12 = (bf16[512,512]{1,0:T(8,128)(2,1)S(1)}, bf16[512,512]{1,0:T(8,128)(2,1)S(1)}, u32[]{:S(2)}, u32[]{:S(2)}) collective-permute-start(bf16[512,512]{1,0:T(8,128)(2,1)S(1)} %pad_maximum_fusion.2), channel_id=1, source_target_pairs={{0,8},{4,12},{8,0},{12,4},{1,9},{5,13},{9,1},{13,5},{2,10},{6,14},... | collective-permute-start | bytes 1572872 | tf_op jit(solution)/shard_map/ppermute | solution.py:295
  87.0 1.6 %collective-permute-start.14 = (bf16[512,512]{1,0:T(8,128)(2,1)S(1)}, bf16[512,512]{1,0:T(8,128)(2,1)S(1)}, u32[]{:S(2)}, u32[]{:S(2)}) collective-permute-start(bf16[512,512]{1,0:T(8,128)(2,1)S(1)} %pad_maximum_fusion.3), channel_id=1, source_target_pairs={{0,4},{4,0},{8,12},{12,8},{1,5},{5,1},{9,13},{13,9},{2,6},{6,2},{1... | collective-permute-start | bytes 1572872 | tf_op jit(solution)/shard_map/ppermute | solution.py:295
  89.8 8.6 %collective-permute-done.6 = bf16[512,512]{1,0:T(8,128)(2,1)S(1)} collective-permute-done((bf16[512,512]{1,0:T(8,128)(2,1)S(1)}, bf16[512,512]{1,0:T(8,128)(2,1)S(1)}, u32[]{:S(2)}, u32[]{:S(2)}) %collective-permute-start.6) | collective-permute-done | bytes 524320 | tf_op jit(solution)/shard_map/ppermute | solution.py:295
  98.7 1.6 %collective-permute-start.9 = (bf16[256,512]{1,0:T(8,128)(2,1)S(1)}, bf16[256,512]{1,0:T(8,128)(2,1)S(1)}, u32[]{:S(2)}, u32[]{:S(2)}) collective-permute-start(bf16[256,512]{1,0:T(8,128)(2,1)S(1)} %fusion.12), channel_id=1, source_target_pairs={{0,8},{4,12},{8,0},{12,4},{1,9},{5,13},{9,1},{13,5},{2,10},{6,14},... | collective-permute-start | bytes 786440 | tf_op jit(solution)/shard_map/ppermute | solution.py:295
  100.6 0.9 collective-permute-start.13
  101.5 8.1 %collective-permute-done.14 = bf16[512,512]{1,0:T(8,128)(2,1)S(1)} collective-permute-done((bf16[512,512]{1,0:T(8,128)(2,1)S(1)}, bf16[512,512]{1,0:T(8,128)(2,1)S(1)}, u32[]{:S(2)}, u32[]{:S(2)}) %collective-permute-start.14) | collective-permute-done | bytes 524320 | tf_op jit(solution)/shard_map/ppermute | solution.py:295
  109.9 1.6 %collective-permute-start.15 = (bf16[256,512]{1,0:T(8,128)(2,1)S(1)}, bf16[256,512]{1,0:T(8,128)(2,1)S(1)}, u32[]{:S(2)}, u32[]{:S(2)}) collective-permute-start(bf16[256,512]{1,0:T(8,128)(2,1)S(1)} %fusion.14), channel_id=1, source_target_pairs={{0,8},{4,12},{8,0},{12,4},{1,9},{5,13},{9,1},{13,5},{2,10},{6,14},... | collective-permute-start | bytes 786440 | tf_op jit(solution)/shard_map/ppermute | solution.py:295
  111.8 0.9 collective-permute-start.17
  112.7 3.6 %collective-permute-done.9 = bf16[256,512]{1,0:T(8,128)(2,1)S(1)} collective-permute-done((bf16[256,512]{1,0:T(8,128)(2,1)S(1)}, bf16[256,512]{1,0:T(8,128)(2,1)S(1)}, u32[]{:S(2)}, u32[]{:S(2)}) %collective-permute-start.9) | collective-permute-done | bytes 262176 | tf_op jit(solution)/shard_map/ppermute | solution.py:295
  117.4 3.8 %collective-permute-done.15 = bf16[256,512]{1,0:T(8,128)(2,1)S(1)} collective-permute-done((bf16[256,512]{1,0:T(8,128)(2,1)S(1)}, bf16[256,512]{1,0:T(8,128)(2,1)S(1)}, u32[]{:S(2)}, u32[]{:S(2)}) %collective-permute-start.15) | collective-permute-done | bytes 262176 | tf_op jit(solution)/shard_map/ppermute | solution.py:295
  122.1 1.0 pad_maximum_fusion
  (74 shorter events, 13.3 us)
Async XLA Ops:
  3.5 15.8 %copy-start.7 = (f32[16]{0:T(128)S(1)}, f32[16]{0:T(128)}, u32[]{:S(2)}) copy-start(f32[16]{0:T(128)} %param.15) | copy-start | bytes 196
  15.6 4.4 %collective-permute-start = (bf16[128,1024]{1,0:T(8,128)(2,1)}, bf16[128,1024]{1,0:T(8,128)(2,1)S(1)}, u32[]{:S(2)}, u32[]{:S(2)}) collective-permute-start(bf16[128,1024]{1,0:T(8,128)(2,1)} %get-tuple-element.21), channel_id=1, source_target_pairs={{0,16},{1,17},{2,18},{3,19},{4,20},{5,21},{6,22},{7,23},{8,24},{9,... | collective-permute-start | bytes 786440 | tf_op jit(solution)/shard_map/ppermute | solution.py:231
  18.0 3.6 %collective-permute-start.1 = (bf16[128,1024]{1,0:T(8,128)(2,1)}, bf16[128,1024]{1,0:T(8,128)(2,1)S(1)}, u32[]{:S(2)}, u32[]{:S(2)}) collective-permute-start(bf16[128,1024]{1,0:T(8,128)(2,1)} %get-tuple-element.22), channel_id=1, source_target_pairs={{16,0},{17,1},{18,2},{19,3},{20,4},{21,5},{22,6},{23,7},{24,8},{25... | collective-permute-start | bytes 786440 | tf_op jit(solution)/shard_map/ppermute | solution.py:231
  20.0 1.6 %copy-start.5 = (bf16[128,1024]{1,0:T(8,128)(2,1)}, bf16[128,1024]{1,0:T(8,128)(2,1)S(1)}, u32[]{:S(2)}) copy-start(bf16[128,1024]{1,0:T(8,128)(2,1)S(1)} %collective-permute-done.cf_ref) | copy-start | bytes 786436
  21.6 0.7 copy-start.6
  46.4 31.4 %copy-start.3 = (bf16[256,1024]{1,0:T(8,128)(2,1)S(1)}, bf16[256,1024]{1,0:T(8,128)(2,1)}, u32[]{:S(2)}) copy-start(bf16[256,1024]{1,0:T(8,128)(2,1)} %get-tuple-element.23) | copy-start | bytes 1572868
  47.2 6.3 %collective-permute-start.10 = (f32[1,1024]{1,0:T(1,128)S(1)}, f32[1,1024]{1,0:T(1,128)S(1)}, u32[]{:S(2)}, u32[]{:S(2)}) collective-permute-start(f32[1,1024]{1,0:T(1,128)S(1)} %pad_maximum_fusion.5), channel_id=1, source_target_pairs={{0,8},{4,12},{8,0},{12,4},{1,9},{5,13},{9,1},{13,5},{2,10},{6,14},... | collective-permute-start | bytes 12296 | tf_op jit(solution)/shard_map/ppermute | solution.py:303
  51.9 28.0 %copy-start.2 = (bf16[256,1024]{1,0:T(8,128)(2,1)S(1)}, bf16[256,1024]{1,0:T(8,128)(2,1)}, u32[]{:S(2)}) copy-start(bf16[256,1024]{1,0:T(8,128)(2,1)} %get-tuple-element.28) | copy-start | bytes 1572868
  51.9 25.3 %collective-permute-start.2 = (bf16[512,512]{1,0:T(8,128)(2,1)}, bf16[512,512]{1,0:T(8,128)(2,1)S(1)}, u32[]{:S(2)}, u32[]{:S(2)}) collective-permute-start(bf16[512,512]{1,0:T(8,128)(2,1)} %get-tuple-element.34), channel_id=1, source_target_pairs={{0,4},{4,0},{8,12},{12,8},{1,5},{5,1},{9,13},{13,9},{2,6},{6,2},{1... | collective-permute-start | bytes 1572872 | tf_op jit(solution)/shard_map/ppermute | solution.py:175
  53.4 23.9 %collective-permute-start.4 = (bf16[512,512]{1,0:T(8,128)(2,1)}, bf16[512,512]{1,0:T(8,128)(2,1)S(1)}, u32[]{:S(2)}, u32[]{:S(2)}) collective-permute-start(bf16[512,512]{1,0:T(8,128)(2,1)} %get-tuple-element.35), channel_id=1, source_target_pairs={{0,12},{4,8},{8,4},{12,0},{1,13},{5,9},{9,5},{13,1},{2,14},{6,10},... | collective-permute-start | bytes 1572872 | tf_op jit(solution)/shard_map/ppermute | solution.py:175
  53.4 23.8 %collective-permute-start.11 = (f32[1,1024]{1,0:T(1,128)S(1)}, f32[1,1024]{1,0:T(1,128)S(1)}, u32[]{:S(2)}, u32[]{:S(2)}) collective-permute-start(f32[1,1024]{1,0:T(1,128)S(1)} %fusion.125), channel_id=1, source_target_pairs={{0,4},{4,0},{8,12},{12,8},{1,5},{5,1},{9,13},{13,9},{2,6},{6,2},{1... | collective-permute-start | bytes 12296 | tf_op jit(solution)/shard_map/ppermute | solution.py:303
  55.5 24.1 %collective-permute-start.7 = (bf16[512,512]{1,0:T(8,128)(2,1)S(1)}, bf16[512,512]{1,0:T(8,128)(2,1)S(1)}, u32[]{:S(2)}, u32[]{:S(2)}) collective-permute-start(bf16[512,512]{1,0:T(8,128)(2,1)S(1)} %get-tuple-element.33), channel_id=1, source_target_pairs={{0,8},{4,12},{8,0},{12,4},{1,9},{5,13},{9,1},{13,5},{2,10},{6,14},... | collective-permute-start | bytes 1572872 | tf_op jit(solution)/shard_map/ppermute | solution.py:175
  77.2 5.6 %collective-permute-start.3 = (bf16[512,512]{1,0:T(8,128)(2,1)S(1)}, bf16[512,512]{1,0:T(8,128)(2,1)S(1)}, u32[]{:S(2)}, u32[]{:S(2)}) collective-permute-start(bf16[512,512]{1,0:T(8,128)(2,1)S(1)} %collective-permute-done.2), channel_id=1, source_target_pairs={{0,16},{16,0},{1,17},{17,1},{2,18},{18,2},{3,19},{19,3},{4,20},{20... | collective-permute-start | bytes 1572872 | tf_op jit(solution)/shard_map/ppermute | solution.py:181
  77.3 5.8 %collective-permute-start.5 = (bf16[512,512]{1,0:T(8,128)(2,1)S(1)}, bf16[512,512]{1,0:T(8,128)(2,1)S(1)}, u32[]{:S(2)}, u32[]{:S(2)}) collective-permute-start(bf16[512,512]{1,0:T(8,128)(2,1)S(1)} %collective-permute-done.4), channel_id=1, source_target_pairs={{0,16},{16,0},{1,17},{17,1},{2,18},{18,2},{3,19},{19,3},{4,20},{20... | collective-permute-start | bytes 1572872 | tf_op jit(solution)/shard_map/ppermute | solution.py:181
  79.9 1.0 copy-start.1
  79.9 4.4 %collective-permute-start.8 = (bf16[512,512]{1,0:T(8,128)(2,1)S(1)}, bf16[512,512]{1,0:T(8,128)(2,1)S(1)}, u32[]{:S(2)}, u32[]{:S(2)}) collective-permute-start(bf16[512,512]{1,0:T(8,128)(2,1)S(1)} %collective-permute-done.7), channel_id=1, source_target_pairs={{0,16},{16,0},{1,17},{17,1},{2,18},{18,2},{3,19},{19,3},{4,20},{20... | collective-permute-start | bytes 1572872 | tf_op jit(solution)/shard_map/ppermute | solution.py:181
  80.9 1.1 copy-start
  83.5 14.9 %collective-permute-start.6 = (bf16[512,512]{1,0:T(8,128)(2,1)S(1)}, bf16[512,512]{1,0:T(8,128)(2,1)S(1)}, u32[]{:S(2)}, u32[]{:S(2)}) collective-permute-start(bf16[512,512]{1,0:T(8,128)(2,1)S(1)} %pad_maximum_fusion.1), channel_id=1, source_target_pairs={{0,4},{4,0},{8,12},{12,8},{1,5},{5,1},{9,13},{13,9},{2,6},{6,2},{1... | collective-permute-start | bytes 1572872 | tf_op jit(solution)/shard_map/ppermute | solution.py:295
  84.7 15.6 %collective-permute-start.12 = (bf16[512,512]{1,0:T(8,128)(2,1)S(1)}, bf16[512,512]{1,0:T(8,128)(2,1)S(1)}, u32[]{:S(2)}, u32[]{:S(2)}) collective-permute-start(bf16[512,512]{1,0:T(8,128)(2,1)S(1)} %pad_maximum_fusion.2), channel_id=1, source_target_pairs={{0,8},{4,12},{8,0},{12,4},{1,9},{5,13},{9,1},{13,5},{2,10},{6,14},... | collective-permute-start | bytes 1572872 | tf_op jit(solution)/shard_map/ppermute | solution.py:295
  87.0 22.6 %collective-permute-start.14 = (bf16[512,512]{1,0:T(8,128)(2,1)S(1)}, bf16[512,512]{1,0:T(8,128)(2,1)S(1)}, u32[]{:S(2)}, u32[]{:S(2)}) collective-permute-start(bf16[512,512]{1,0:T(8,128)(2,1)S(1)} %pad_maximum_fusion.3), channel_id=1, source_target_pairs={{0,4},{4,0},{8,12},{12,8},{1,5},{5,1},{9,13},{13,9},{2,6},{6,2},{1... | collective-permute-start | bytes 1572872 | tf_op jit(solution)/shard_map/ppermute | solution.py:295
  89.2 22.3 %collective-permute-start.16 = (bf16[512,512]{1,0:T(8,128)(2,1)S(1)}, bf16[512,512]{1,0:T(8,128)(2,1)S(1)}, u32[]{:S(2)}, u32[]{:S(2)}) collective-permute-start(bf16[512,512]{1,0:T(8,128)(2,1)S(1)} %pad_maximum_fusion.4), channel_id=1, source_target_pairs={{0,8},{4,12},{8,0},{12,4},{1,9},{5,13},{9,1},{13,5},{2,10},{6,14},... | collective-permute-start | bytes 1572872 | tf_op jit(solution)/shard_map/ppermute | solution.py:295
  98.7 17.7 %collective-permute-start.9 = (bf16[256,512]{1,0:T(8,128)(2,1)S(1)}, bf16[256,512]{1,0:T(8,128)(2,1)S(1)}, u32[]{:S(2)}, u32[]{:S(2)}) collective-permute-start(bf16[256,512]{1,0:T(8,128)(2,1)S(1)} %fusion.12), channel_id=1, source_target_pairs={{0,8},{4,12},{8,0},{12,4},{1,9},{5,13},{9,1},{13,5},{2,10},{6,14},... | collective-permute-start | bytes 786440 | tf_op jit(solution)/shard_map/ppermute | solution.py:295
  100.3 16.1 %copy-start.4 = (bf16[4096,512]{1,0:T(8,128)(2,1)S(1)}, bf16[4096,512]{1,0:T(8,128)(2,1)}, u32[]{:S(2)}) copy-start(bf16[4096,512]{1,0:T(8,128)(2,1)} %param.17) | copy-start | bytes 12582916
  100.6 16.3 %collective-permute-start.13 = (bf16[256,512]{1,0:T(8,128)(2,1)S(1)}, bf16[256,512]{1,0:T(8,128)(2,1)S(1)}, u32[]{:S(2)}, u32[]{:S(2)}) collective-permute-start(bf16[256,512]{1,0:T(8,128)(2,1)S(1)} %fusion.13), channel_id=1, source_target_pairs={{0,4},{4,0},{8,12},{12,8},{1,5},{5,1},{9,13},{13,9},{2,6},{6,2},{1... | collective-permute-start | bytes 786440 | tf_op jit(solution)/shard_map/ppermute | solution.py:295
  109.9 11.3 %collective-permute-start.15 = (bf16[256,512]{1,0:T(8,128)(2,1)S(1)}, bf16[256,512]{1,0:T(8,128)(2,1)S(1)}, u32[]{:S(2)}, u32[]{:S(2)}) collective-permute-start(bf16[256,512]{1,0:T(8,128)(2,1)S(1)} %fusion.14), channel_id=1, source_target_pairs={{0,8},{4,12},{8,0},{12,4},{1,9},{5,13},{9,1},{13,5},{2,10},{6,14},... | collective-permute-start | bytes 786440 | tf_op jit(solution)/shard_map/ppermute | solution.py:295
  111.8 9.8 %collective-permute-start.17 = (bf16[256,512]{1,0:T(8,128)(2,1)S(1)}, bf16[256,512]{1,0:T(8,128)(2,1)S(1)}, u32[]{:S(2)}, u32[]{:S(2)}) collective-permute-start(bf16[256,512]{1,0:T(8,128)(2,1)S(1)} %fusion.15), channel_id=1, source_target_pairs={{0,4},{4,0},{8,12},{12,8},{1,5},{5,1},{9,13},{13,9},{2,6},{6,2},{1... | collective-permute-start | bytes 786440 | tf_op jit(solution)/shard_map/ppermute | solution.py:295

commit v3 on v2

--- a/solution.py
+++ b/solution.py
@@ -92,7 +92,7 @@
             weigh = nn(cols, spread[place])
             xw = (x_ref[pl.ds(at, Q), :].astype(F32) * weigh).astype(BF16)
             decay = nn(cols[:16], spread[2 + place])[:8]
-            state[...] = state[...] * decay[:1] + tn(b_ref[pl.ds(at, Q), :], xw)
+            state[...] = state[...] * decay[:1] + tn(b_ref[0, pl.ds(at, Q), :], xw)
             dec[...] = dec[...] * decay
         return 0
 
@@ -223,7 +223,7 @@
         name="scan_states",
     )
     ent_f, ent_b, dec, end_f, end_b, tot = states(
-        ssm_input, proj_forward[0], proj_backward[0], raw, params
+        ssm_input, proj_forward, proj_backward, raw, params
     )
 
     def carried(end, decay, step):
@@ -296,7 +296,7 @@
             for r, part in zip(going, jnp.split(got, len(going), axis=0)):
                 parts[r ^ bit] = parts[r ^ bit] + part.astype(F32)
         owned.append(parts[0])
-        squares.append(sums[0:1])
+        squares.append(sums)
     squares = jnp.concatenate(squares, axis=1)
     for bit in bits:
         perm = [(i, i ^ bit) for i in range(n_chan)]

time: 124 us -> 113 us (0.911)
  waiting for transfers between devices: 47.1 us -> 40.2 us
  starting transfers between devices: 21 us -> 18.8 us
  local copies, waits for them, and re-layouts: 10.3 us -> 8.56 us
    ppermute x2, waiting for transfers between devices: 20.2 us -> 5.81 us  [body(): squares = squares + lax.ppermute(squares, 'chan', perm)]
    ppermute x3, waiting for transfers between devices: 1.13 us -> 9.33 us  [body(): pieces[k] = lax.ppermute(part, 'chan', [(i, i ^ k) for i in range(n_chan)])]
    ppermute x2, starting transfers between devices: 4.37 us -> 1.51 us  [body(): squares = squares + lax.ppermute(squares, 'chan', perm)]
    slice x4 -> x0, local copies, waits for them, and re-layouts: 2.85 us -> none  [body(): squares.append(sums[0:1])]
    unnamed x16 -> x19, local copies, waits for them, and re-layouts: 0.86 us -> 3.05 us
    squeeze x1 -> x0, local copies, waits for them, and re-layouts: 1.87 us -> none  [body(): proj_backward[0]]
    ppermute x2, waiting for transfers between devices: 1.63 us -> 0.01 us  [carried(): out = lax.ppermute(end, 'seq', pairs)]
    ppermute x3, starting transfers between devices: 3.01 us -> 4.31 us  [body(): pieces[k] = lax.ppermute(part, 'chan', [(i, i ^ k) for i in range(n_chan)])]
  transfers between devices with their start and end apart: 18 -> 18, of which waited for: 7 -> 9; matrix products, arithmetic and copies ran while one was open for 10% -> 13% of each run, Pallas kernels for 0% -> 20%
where the time goes in v3:
time: 113 us; the launch traced here: 112 us
  waiting for transfers between devices  40.2 us (36%)
  Pallas kernels  34.1 us (30%)
  starting transfers between devices  18.8 us (17%)
  matrix products  9.02 us (8%)
  local copies, waits for them, and re-layouts  8.56 us (8%)
  other arithmetic  1.21 us (1%)
    ppermute x8, waiting for transfers between devices, body(): got = lax.ppermute(got, 'chan', perm)  25.1 us
    pallas_call x4, Pallas kernels, body(): outputs(ssm_input, gate_z, proj_forward, proj_backward, raw, params, skip...  22 us
    pallas_call x1, Pallas kernels, body(): states(ssm_input, proj_forward, proj_backward, raw, params)  12.2 us
    ppermute x3, waiting for transfers between devices, body(): pieces[k] = lax.ppermute(part, 'chan', [(i, i ^ k) for i in range(n_chan)])  9.33 us
    ppermute x8, starting transfers between devices, body(): got = lax.ppermute(got, 'chan', perm)  8.57 us
    dot_general x24, matrix products, product(): jnp.dot(lax.dynamic_slice(gated, (0, at), (gated.shape[0], share)), part,...  7.14 us
    ppermute x2, waiting for transfers between devices, body(): squares = squares + lax.ppermute(squares, 'chan', perm)  5.81 us
    ppermute x3, starting transfers between devices, body(): pieces[k] = lax.ppermute(part, 'chan', [(i, i ^ k) for i in range(n_chan)])  4.31 us
  transfers between devices with their start and end apart: 18, of which 9 were waited for; matrix products, arithmetic and copies ran while one was open for 13% of the time, Pallas kernels for 20%

profile of v3, /device:TPU:0, one launch (start us, length us, event | category | flops | bytes accessed | tf_op | source)
XLA Modules:
  0.0 112.5 jit_solution(5140177105605467187)
XLA Ops:
  0.0 0.8 slice_reduce_fusion.1
  1.0 0.7 copy.15.hp_ref
  1.6 12.2 %scan_states.1 = (bf16[8,128,1024]{2,1,0:T(8,128)(2,1)}, bf16[8,128,1024]{2,1,0:T(8,128)(2,1)}, f32[8,16,1024]{2,1,0:T(8,128)}, bf16[128,1024]{1,0:T(8,128)(2,1)...) custom-call(bf16[1024,1024]{1,0:T(8,128)(2,1)} %x_ref.9, bf16[2,1024,128]{2,1,0:T(8,128)(2,1)} %pf_ref.7, ...), custom_call_target="tpu_custom_call" | custom-call | flops 4000000000 | bytes 8388608 | tf_op jit(solution)/shard_map/scan_states/pallas_call | solution.py:225
  13.8 2.5 %collective-permute-start = (bf16[128,1024]{1,0:T(8,128)(2,1)}, bf16[128,1024]{1,0:T(8,128)(2,1)S(1)}, u32[]{:S(2)}, u32[]{:S(2)}) collective-permute-start(bf16[128,1024]{1,0:T(8,128)(2,1)} %get-tuple-element.21), channel_id=1, source_target_pairs={{0,16},{1,17},{2,18},{3,19},{4,20},{5,21},{6,22},{7,23},{8,24},{9,... | collective-permute-start | bytes 786440 | tf_op jit(solution)/shard_map/ppermute | solution.py:231
  16.4 1.3 %collective-permute-start.1 = (bf16[128,1024]{1,0:T(8,128)(2,1)}, bf16[128,1024]{1,0:T(8,128)(2,1)S(1)}, u32[]{:S(2)}, u32[]{:S(2)}) collective-permute-start(bf16[128,1024]{1,0:T(8,128)(2,1)} %get-tuple-element.22), channel_id=1, source_target_pairs={{16,0},{17,1},{18,2},{19,3},{20,4},{21,5},{22,6},{23,7},{24,8},{25... | collective-permute-start | bytes 786440 | tf_op jit(solution)/shard_map/ppermute | solution.py:231
  17.7 2.5 %constant_dynamic-slice_fusion = (bf16[512,512]{1,0:T(8,128)(2,1)S(1)}, bf16[512,512]{1,0:T(8,128)(2,1)}, bf16[512,512]{1,0:T(8,128)(2,1)}) fusion(bf16[4096,512]{1,0:T(8,128)(2,1)} %param.17, s32[]{:T(128)S(6)} %select_n.29, s32[]{:T(128)S(6)} %select_n.25, s32[]{:T(128)S(6)} %select_n.28), kind=kLoop, calls=%fused_computation.121 | loop fusion | bytes 3145740 | tf_op jit(solution)/shard_map/dynamic_slice | solution.py:174
  20.2 2.3 %collective-permute-start.2 = (bf16[512,512]{1,0:T(8,128)(2,1)}, bf16[512,512]{1,0:T(8,128)(2,1)S(1)}, u32[]{:S(2)}, u32[]{:S(2)}) collective-permute-start(bf16[512,512]{1,0:T(8,128)(2,1)} %get-tuple-element.34), channel_id=1, source_target_pairs={{0,4},{4,0},{8,12},{12,8},{1,5},{5,1},{9,13},{13,9},{2,6},{6,2},{1... | collective-permute-start | bytes 1572872 | tf_op jit(solution)/shard_map/ppermute | solution.py:175
  22.5 1.5 %collective-permute-start.4 = (bf16[512,512]{1,0:T(8,128)(2,1)}, bf16[512,512]{1,0:T(8,128)(2,1)S(1)}, u32[]{:S(2)}, u32[]{:S(2)}) collective-permute-start(bf16[512,512]{1,0:T(8,128)(2,1)} %get-tuple-element.35), channel_id=1, source_target_pairs={{0,12},{4,8},{8,4},{12,0},{1,13},{5,9},{9,5},{13,1},{2,14},{6,10},... | collective-permute-start | bytes 1572872 | tf_op jit(solution)/shard_map/ppermute | solution.py:175
  24.0 0.6 dynamic_update_slice.3.skip_ref
  24.6 0.7 copy-done.5
  25.4 5.5 %scan_outputs.4 = (bf16[256,1024]{1,0:T(8,128)(2,1)}, f32[8,256]{1,0:T(8,128)}) custom-call(bf16[1024,1024]{1,0:T(8,128)(2,1)} %x_ref.9, bf16[1024,1024]{1,0:T(8,128)(2,1)} %z_ref.7, bf16[2,1024,128]{2,1,0:T(8,128)(2,1)} %pf_ref.7, bf16[2,1024,128]{2,1,0:T(8,128)(2,1)} %pb_ref.7, f32[32,1024]{1,0:T(8,128)} %bitcast.40, f32[32,2]{1,0:T(8,128)} %copy.15.hp_ref, ...), custom_call_target="tpu_custom_call" | custom-call | flops 4000000000 | bytes 8388608 | tf_op jit(solution)/shard_map/scan_outputs/pallas_call | solution.py:284
  30.9 0.7 constant_dynamic-update-slice_fusion.3
  31.6 5.5 %scan_outputs.5 = (bf16[256,1024]{1,0:T(8,128)(2,1)}, f32[8,256]{1,0:T(8,128)}) custom-call(bf16[1024,1024]{1,0:T(8,128)(2,1)} %x_ref.9, bf16[1024,1024]{1,0:T(8,128)(2,1)} %z_ref.7, bf16[2,1024,128]{2,1,0:T(8,128)(2,1)} %pf_ref.7, bf16[2,1024,128]{2,1,0:T(8,128)(2,1)} %pb_ref.7, f32[32,1024]{1,0:T(8,128)} %bitcast.41, f32[32,2]{1,0:T(8,128)} %copy.15.hp_ref, ...), custom_call_target="tpu_custom_call" | custom-call | flops 4000000000 | bytes 8388608 | tf_op jit(solution)/shard_map/scan_outputs/pallas_call | solution.py:284
  37.1 0.7 constant_dynamic-update-slice_fusion.2
  37.8 5.5 %scan_outputs.6 = (bf16[256,1024]{1,0:T(8,128)(2,1)}, f32[8,256]{1,0:T(8,128)}) custom-call(bf16[1024,1024]{1,0:T(8,128)(2,1)} %x_ref.9, bf16[1024,1024]{1,0:T(8,128)(2,1)} %z_ref.7, bf16[2,1024,128]{2,1,0:T(8,128)(2,1)} %pf_ref.7, bf16[2,1024,128]{2,1,0:T(8,128)(2,1)} %pb_ref.7, f32[32,1024]{1,0:T(8,128)} %bitcast.42, f32[32,2]{1,0:T(8,128)} %copy.15.hp_ref, ...), custom_call_target="tpu_custom_call" | custom-call | flops 4000000000 | bytes 8388608 | tf_op jit(solution)/shard_map/scan_outputs/pallas_call | solution.py:284
  43.3 0.7 constant_dynamic-update-slice_fusion.1
  44.0 5.5 %scan_outputs.7 = (bf16[256,1024]{1,0:T(8,128)(2,1)}, f32[8,256]{1,0:T(8,128)}) custom-call(bf16[1024,1024]{1,0:T(8,128)(2,1)} %x_ref.9, bf16[1024,1024]{1,0:T(8,128)(2,1)} %z_ref.7, bf16[2,1024,128]{2,1,0:T(8,128)(2,1)} %pf_ref.7, bf16[2,1024,128]{2,1,0:T(8,128)(2,1)} %pb_ref.7, f32[32,1024]{1,0:T(8,128)} %bitcast.43, f32[32,2]{1,0:T(8,128)} %copy.15.hp_ref, ...), custom_call_target="tpu_custom_call" | custom-call | flops 4000000000 | bytes 8388608 | tf_op jit(solution)/shard_map/scan_outputs/pallas_call | solution.py:284
  49.5 0.8 constant_dynamic-update-slice_fusion
  50.3 3.9 %collective-permute-done.10 = f32[8,1024]{1,0:T(8,128)S(1)} collective-permute-done((f32[8,1024]{1,0:T(8,128)S(1)}, f32[8,1024]{1,0:T(8,128)S(1)}, u32[]{:S(2)}, u32[]{:S(2)}) %collective-permute-start.10) | collective-permute-done | bytes 32800 | tf_op jit(solution)/shard_map/ppermute | solution.py:303
  54.2 1.5 %collective-permute-start.11 = (f32[8,1024]{1,0:T(8,128)S(1)}, f32[8,1024]{1,0:T(8,128)S(1)}, u32[]{:S(2)}, u32[]{:S(2)}) collective-permute-start(f32[8,1024]{1,0:T(8,128)S(1)} %add.164), channel_id=1, source_target_pairs={{0,4},{4,0},{8,12},{12,8},{1,5},{5,1},{9,13},{13,9},{2,6},{6,2},{1... | collective-permute-start | bytes 98312 | tf_op jit(solution)/shard_map/ppermute | solution.py:303
  56.2 1.9 %collective-permute-done.11 = f32[8,1024]{1,0:T(8,128)S(1)} collective-permute-done((f32[8,1024]{1,0:T(8,128)S(1)}, f32[8,1024]{1,0:T(8,128)S(1)}, u32[]{:S(2)}, u32[]{:S(2)}) %collective-permute-start.11) | collective-permute-done | bytes 32800 | tf_op jit(solution)/shard_map/ppermute | solution.py:303
  59.3 9.3 %collective-permute-done.7 = bf16[512,512]{1,0:T(8,128)(2,1)S(1)} collective-permute-done((bf16[512,512]{1,0:T(8,128)(2,1)S(1)}, bf16[512,512]{1,0:T(8,128)(2,1)S(1)}, u32[]{:S(2)}, u32[]{:S(2)}) %collective-permute-start.7) | collective-permute-done | bytes 524320 | tf_op jit(solution)/shard_map/ppermute | solution.py:175
  73.9 0.9 collective-permute-start.12
  75.5 1.2 %collective-permute-start.14 = (bf16[512,512]{1,0:T(8,128)(2,1)S(1)}, bf16[512,512]{1,0:T(8,128)(2,1)S(1)}, u32[]{:S(2)}, u32[]{:S(2)}) collective-permute-start(bf16[512,512]{1,0:T(8,128)(2,1)S(1)} %pad_maximum_fusion.3), channel_id=1, source_target_pairs={{0,4},{4,0},{8,12},{12,8},{1,5},{5,1},{9,13},{13,9},{2,6},{6,2},{1... | collective-permute-start | bytes 1572872 | tf_op jit(solution)/shard_map/ppermute | solution.py:295
  77.3 1.6 %collective-permute-start.16 = (bf16[512,512]{1,0:T(8,128)(2,1)S(1)}, bf16[512,512]{1,0:T(8,128)(2,1)S(1)}, u32[]{:S(2)}, u32[]{:S(2)}) collective-permute-start(bf16[512,512]{1,0:T(8,128)(2,1)S(1)} %pad_maximum_fusion.4), channel_id=1, source_target_pairs={{0,8},{4,12},{8,0},{12,4},{1,9},{5,13},{9,1},{13,5},{2,10},{6,14},... | collective-permute-start | bytes 1572872 | tf_op jit(solution)/shard_map/ppermute | solution.py:295
  78.9 8.6 %collective-permute-done.6 = bf16[512,512]{1,0:T(8,128)(2,1)S(1)} collective-permute-done((bf16[512,512]{1,0:T(8,128)(2,1)S(1)}, bf16[512,512]{1,0:T(8,128)(2,1)S(1)}, u32[]{:S(2)}, u32[]{:S(2)}) %collective-permute-start.6) | collective-permute-done | bytes 524320 | tf_op jit(solution)/shard_map/ppermute | solution.py:295
  89.1 1.6 %collective-permute-start.13 = (bf16[256,512]{1,0:T(8,128)(2,1)S(1)}, bf16[256,512]{1,0:T(8,128)(2,1)S(1)}, u32[]{:S(2)}, u32[]{:S(2)}) collective-permute-start(bf16[256,512]{1,0:T(8,128)(2,1)S(1)} %fusion.13), channel_id=1, source_target_pairs={{0,4},{4,0},{8,12},{12,8},{1,5},{5,1},{9,13},{13,9},{2,6},{6,2},{1... | collective-permute-start | bytes 786440 | tf_op jit(solution)/shard_map/ppermute | solution.py:295
  90.6 8.1 %collective-permute-done.14 = bf16[512,512]{1,0:T(8,128)(2,1)S(1)} collective-permute-done((bf16[512,512]{1,0:T(8,128)(2,1)S(1)}, bf16[512,512]{1,0:T(8,128)(2,1)S(1)}, u32[]{:S(2)}, u32[]{:S(2)}) %collective-permute-start.14) | collective-permute-done | bytes 524320 | tf_op jit(solution)/shard_map/ppermute | solution.py:295
  100.3 1.6 %collective-permute-start.17 = (bf16[256,512]{1,0:T(8,128)(2,1)S(1)}, bf16[256,512]{1,0:T(8,128)(2,1)S(1)}, u32[]{:S(2)}, u32[]{:S(2)}) collective-permute-start(bf16[256,512]{1,0:T(8,128)(2,1)S(1)} %fusion.15), channel_id=1, source_target_pairs={{0,4},{4,0},{8,12},{12,8},{1,5},{5,1},{9,13},{13,9},{2,6},{6,2},{1... | collective-permute-start | bytes 786440 | tf_op jit(solution)/shard_map/ppermute | solution.py:295
  101.8 3.8 %collective-permute-done.9 = bf16[256,512]{1,0:T(8,128)(2,1)S(1)} collective-permute-done((bf16[256,512]{1,0:T(8,128)(2,1)S(1)}, bf16[256,512]{1,0:T(8,128)(2,1)S(1)}, u32[]{:S(2)}, u32[]{:S(2)}) %collective-permute-start.9) | collective-permute-done | bytes 262176 | tf_op jit(solution)/shard_map/ppermute | solution.py:295
  106.6 3.9 %collective-permute-done.15 = bf16[256,512]{1,0:T(8,128)(2,1)S(1)} collective-permute-done((bf16[256,512]{1,0:T(8,128)(2,1)S(1)}, bf16[256,512]{1,0:T(8,128)(2,1)S(1)}, u32[]{:S(2)}, u32[]{:S(2)}) %collective-permute-start.15) | collective-permute-done | bytes 262176 | tf_op jit(solution)/shard_map/ppermute | solution.py:295
  111.4 1.0 pad_maximum_fusion
  (72 shorter events, 13.3 us)
Async XLA Ops:
  13.8 10.2 %copy-start.7 = (f32[16]{0:T(128)S(1)}, f32[16]{0:T(128)}, u32[]{:S(2)}) copy-start(f32[16]{0:T(128)} %param.15) | copy-start | bytes 196
  13.8 10.8 %collective-permute-start = (bf16[128,1024]{1,0:T(8,128)(2,1)}, bf16[128,1024]{1,0:T(8,128)(2,1)S(1)}, u32[]{:S(2)}, u32[]{:S(2)}) collective-permute-start(bf16[128,1024]{1,0:T(8,128)(2,1)} %get-tuple-element.21), channel_id=1, source_target_pairs={{0,16},{1,17},{2,18},{3,19},{4,20},{5,21},{6,22},{7,23},{8,24},{9,... | collective-permute-start | bytes 786440 | tf_op jit(solution)/shard_map/ppermute | solution.py:231
  16.4 8.3 %collective-permute-start.1 = (bf16[128,1024]{1,0:T(8,128)(2,1)}, bf16[128,1024]{1,0:T(8,128)(2,1)S(1)}, u32[]{:S(2)}, u32[]{:S(2)}) collective-permute-start(bf16[128,1024]{1,0:T(8,128)(2,1)} %get-tuple-element.22), channel_id=1, source_target_pairs={{16,0},{17,1},{18,2},{19,3},{20,4},{21,5},{22,6},{23,7},{24,8},{25... | collective-permute-start | bytes 786440 | tf_op jit(solution)/shard_map/ppermute | solution.py:231
  20.2 38.0 %collective-permute-start.2 = (bf16[512,512]{1,0:T(8,128)(2,1)}, bf16[512,512]{1,0:T(8,128)(2,1)S(1)}, u32[]{:S(2)}, u32[]{:S(2)}) collective-permute-start(bf16[512,512]{1,0:T(8,128)(2,1)} %get-tuple-element.34), channel_id=1, source_target_pairs={{0,4},{4,0},{8,12},{12,8},{1,5},{5,1},{9,13},{13,9},{2,6},{6,2},{1... | collective-permute-start | bytes 1572872 | tf_op jit(solution)/shard_map/ppermute | solution.py:175
  22.5 35.8 %collective-permute-start.4 = (bf16[512,512]{1,0:T(8,128)(2,1)}, bf16[512,512]{1,0:T(8,128)(2,1)S(1)}, u32[]{:S(2)}, u32[]{:S(2)}) collective-permute-start(bf16[512,512]{1,0:T(8,128)(2,1)} %get-tuple-element.35), channel_id=1, source_target_pairs={{0,12},{4,8},{8,4},{12,0},{1,13},{5,9},{9,5},{13,1},{2,14},{6,10},... | collective-permute-start | bytes 1572872 | tf_op jit(solution)/shard_map/ppermute | solution.py:175
  24.6 0.7 copy-start.5
  24.6 0.8 copy-start.6
  44.0 14.7 %copy-start.3 = (bf16[256,1024]{1,0:T(8,128)(2,1)S(1)}, bf16[256,1024]{1,0:T(8,128)(2,1)}, u32[]{:S(2)}) copy-start(bf16[256,1024]{1,0:T(8,128)(2,1)} %get-tuple-element.23) | copy-start | bytes 1572868
  49.5 19.5 %copy-start.2 = (bf16[256,1024]{1,0:T(8,128)(2,1)S(1)}, bf16[256,1024]{1,0:T(8,128)(2,1)}, u32[]{:S(2)}) copy-start(bf16[256,1024]{1,0:T(8,128)(2,1)} %get-tuple-element.28) | copy-start | bytes 1572868
  50.3 3.9 %collective-permute-start.10 = (f32[8,1024]{1,0:T(8,128)S(1)}, f32[8,1024]{1,0:T(8,128)S(1)}, u32[]{:S(2)}, u32[]{:S(2)}) collective-permute-start(f32[8,1024]{1,0:T(8,128)S(1)} %constant_dynamic-update-slice_fusion), channel_id=1, source_target_pairs={{0,8},{4,12},{8,0},{12,4},{1,9},{5,13},{9,1},{13,5},{2,10},{6,14},... | collective-permute-start | bytes 98312 | tf_op jit(solution)/shard_map/ppermute | solution.py:303
  54.2 3.9 %collective-permute-start.11 = (f32[8,1024]{1,0:T(8,128)S(1)}, f32[8,1024]{1,0:T(8,128)S(1)}, u32[]{:S(2)}, u32[]{:S(2)}) collective-permute-start(f32[8,1024]{1,0:T(8,128)S(1)} %add.164), channel_id=1, source_target_pairs={{0,4},{4,0},{8,12},{12,8},{1,5},{5,1},{9,13},{13,9},{2,6},{6,2},{1... | collective-permute-start | bytes 98312 | tf_op jit(solution)/shard_map/ppermute | solution.py:303
  55.7 13.0 %collective-permute-start.7 = (bf16[512,512]{1,0:T(8,128)(2,1)S(1)}, bf16[512,512]{1,0:T(8,128)(2,1)S(1)}, u32[]{:S(2)}, u32[]{:S(2)}) collective-permute-start(bf16[512,512]{1,0:T(8,128)(2,1)S(1)} %get-tuple-element.33), channel_id=1, source_target_pairs={{0,8},{4,12},{8,0},{12,4},{1,9},{5,13},{9,1},{13,5},{2,10},{6,14},... | collective-permute-start | bytes 1572872 | tf_op jit(solution)/shard_map/ppermute | solution.py:175
  58.2 13.8 %collective-permute-start.3 = (bf16[512,512]{1,0:T(8,128)(2,1)S(1)}, bf16[512,512]{1,0:T(8,128)(2,1)S(1)}, u32[]{:S(2)}, u32[]{:S(2)}) collective-permute-start(bf16[512,512]{1,0:T(8,128)(2,1)S(1)} %collective-permute-done.2), channel_id=1, source_target_pairs={{0,16},{16,0},{1,17},{17,1},{2,18},{18,2},{3,19},{19,3},{4,20},{20... | collective-permute-start | bytes 1572872 | tf_op jit(solution)/shard_map/ppermute | solution.py:181
  58.2 14.0 %collective-permute-start.5 = (bf16[512,512]{1,0:T(8,128)(2,1)S(1)}, bf16[512,512]{1,0:T(8,128)(2,1)S(1)}, u32[]{:S(2)}, u32[]{:S(2)}) collective-permute-start(bf16[512,512]{1,0:T(8,128)(2,1)S(1)} %collective-permute-done.4), channel_id=1, source_target_pairs={{0,16},{16,0},{1,17},{17,1},{2,18},{18,2},{3,19},{19,3},{4,20},{20... | collective-permute-start | bytes 1572872 | tf_op jit(solution)/shard_map/ppermute | solution.py:181
  69.0 1.0 copy-start.1
  69.0 4.5 %collective-permute-start.8 = (bf16[512,512]{1,0:T(8,128)(2,1)S(1)}, bf16[512,512]{1,0:T(8,128)(2,1)S(1)}, u32[]{:S(2)}, u32[]{:S(2)}) collective-permute-start(bf16[512,512]{1,0:T(8,128)(2,1)S(1)} %collective-permute-done.7), channel_id=1, source_target_pairs={{0,16},{16,0},{1,17},{17,1},{2,18},{18,2},{3,19},{19,3},{4,20},{20... | collective-permute-start | bytes 1572872 | tf_op jit(solution)/shard_map/ppermute | solution.py:181
  70.0 1.1 copy-start
  72.6 14.9 %collective-permute-start.6 = (bf16[512,512]{1,0:T(8,128)(2,1)S(1)}, bf16[512,512]{1,0:T(8,128)(2,1)S(1)}, u32[]{:S(2)}, u32[]{:S(2)}) collective-permute-start(bf16[512,512]{1,0:T(8,128)(2,1)S(1)} %pad_maximum_fusion.1), channel_id=1, source_target_pairs={{0,4},{4,0},{8,12},{12,8},{1,5},{5,1},{9,13},{13,9},{2,6},{6,2},{1... | collective-permute-start | bytes 1572872 | tf_op jit(solution)/shard_map/ppermute | solution.py:295
  73.9 14.9 %collective-permute-start.12 = (bf16[512,512]{1,0:T(8,128)(2,1)S(1)}, bf16[512,512]{1,0:T(8,128)(2,1)S(1)}, u32[]{:S(2)}, u32[]{:S(2)}) collective-permute-start(bf16[512,512]{1,0:T(8,128)(2,1)S(1)} %pad_maximum_fusion.2), channel_id=1, source_target_pairs={{0,8},{4,12},{8,0},{12,4},{1,9},{5,13},{9,1},{13,5},{2,10},{6,14},... | collective-permute-start | bytes 1572872 | tf_op jit(solution)/shard_map/ppermute | solution.py:295
  75.5 23.2 %collective-permute-start.14 = (bf16[512,512]{1,0:T(8,128)(2,1)S(1)}, bf16[512,512]{1,0:T(8,128)(2,1)S(1)}, u32[]{:S(2)}, u32[]{:S(2)}) collective-permute-start(bf16[512,512]{1,0:T(8,128)(2,1)S(1)} %pad_maximum_fusion.3), channel_id=1, source_target_pairs={{0,4},{4,0},{8,12},{12,8},{1,5},{5,1},{9,13},{13,9},{2,6},{6,2},{1... | collective-permute-start | bytes 1572872 | tf_op jit(solution)/shard_map/ppermute | solution.py:295
  77.3 22.7 %collective-permute-start.16 = (bf16[512,512]{1,0:T(8,128)(2,1)S(1)}, bf16[512,512]{1,0:T(8,128)(2,1)S(1)}, u32[]{:S(2)}, u32[]{:S(2)}) collective-permute-start(bf16[512,512]{1,0:T(8,128)(2,1)S(1)} %pad_maximum_fusion.4), channel_id=1, source_target_pairs={{0,8},{4,12},{8,0},{12,4},{1,9},{5,13},{9,1},{13,5},{2,10},{6,14},... | collective-permute-start | bytes 1572872 | tf_op jit(solution)/shard_map/ppermute | solution.py:295
  87.8 17.8 %collective-permute-start.9 = (bf16[256,512]{1,0:T(8,128)(2,1)S(1)}, bf16[256,512]{1,0:T(8,128)(2,1)S(1)}, u32[]{:S(2)}, u32[]{:S(2)}) collective-permute-start(bf16[256,512]{1,0:T(8,128)(2,1)S(1)} %fusion.12), channel_id=1, source_target_pairs={{0,8},{4,12},{8,0},{12,4},{1,9},{5,13},{9,1},{13,5},{2,10},{6,14},... | collective-permute-start | bytes 786440 | tf_op jit(solution)/shard_map/ppermute | solution.py:295
  88.7 16.9 %copy-start.4 = (bf16[4096,512]{1,0:T(8,128)(2,1)S(1)}, bf16[4096,512]{1,0:T(8,128)(2,1)}, u32[]{:S(2)}) copy-start(bf16[4096,512]{1,0:T(8,128)(2,1)} %param.17) | copy-start | bytes 12582916
  89.1 17.0 %collective-permute-start.13 = (bf16[256,512]{1,0:T(8,128)(2,1)S(1)}, bf16[256,512]{1,0:T(8,128)(2,1)S(1)}, u32[]{:S(2)}, u32[]{:S(2)}) collective-permute-start(bf16[256,512]{1,0:T(8,128)(2,1)S(1)} %fusion.13), channel_id=1, source_target_pairs={{0,4},{4,0},{8,12},{12,8},{1,5},{5,1},{9,13},{13,9},{2,6},{6,2},{1... | collective-permute-start | bytes 786440 | tf_op jit(solution)/shard_map/ppermute | solution.py:295
  99.0 11.4 %collective-permute-start.15 = (bf16[256,512]{1,0:T(8,128)(2,1)S(1)}, bf16[256,512]{1,0:T(8,128)(2,1)S(1)}, u32[]{:S(2)}, u32[]{:S(2)}) collective-permute-start(bf16[256,512]{1,0:T(8,128)(2,1)S(1)} %fusion.14), channel_id=1, source_target_pairs={{0,8},{4,12},{8,0},{12,4},{1,9},{5,13},{9,1},{13,5},{2,10},{6,14},... | collective-permute-start | bytes 786440 | tf_op jit(solution)/shard_map/ppermute | solution.py:295
  100.3 10.6 %collective-permute-start.17 = (bf16[256,512]{1,0:T(8,128)(2,1)S(1)}, bf16[256,512]{1,0:T(8,128)(2,1)S(1)}, u32[]{:S(2)}, u32[]{:S(2)}) collective-permute-start(bf16[256,512]{1,0:T(8,128)(2,1)S(1)} %fusion.15), channel_id=1, source_target_pairs={{0,4},{4,0},{8,12},{12,8},{1,5},{5,1},{9,13},{13,9},{2,6},{6,2},{1... | collective-permute-start | bytes 786440 | tf_op jit(solution)/shard_map/ppermute | solution.py:295
